TPU v7x, 512 devices: a whole 4x8x8 slice. The times are simulated.
512 devices in a mesh: dp: 8 (over z), win: 8 (over y), mp: 8 (over x, core).
Axes of the slice: x: 4, y: 8, z: 8, core: 2. Of those that a mesh axis runs over, the one named last changes fastest.
Arguments:
- tokens: bfloat16 [75264, 768], P(('dp', 'win', 'mp')), may hold values from -6 to 6
- target: bfloat16 [75264, 768], P(('dp', 'win', 'mp')), may hold values from -16 to 16
- regions: int32 [1536, 49], P(('dp', 'win')), may hold values from 0 to 3
- rel_index: int32 [49, 49], replicated, may hold values from 0 to 168
- layer_norm_gain: float32 [768], replicated, may hold values from 0.5 to 1.5
- bias_table: float32 [169, 24], P(None, 'mp'), may hold values from -5 to 330
- w_qkv: bfloat16 [3, 768, 768], P(None, 'mp'), may hold values from -0.21875 to 0.21875
- w_proj: bfloat16 [768, 768], P('mp'), may hold values from -0.21875 to 0.21875
Outputs:
- input_gradient: float32 [75264, 768], P(('dp', 'win', 'mp'))
- grad_qkv: float32 [3, 768, 768], P(None, 'mp', ('dp', 'win'))
- grad_proj: float32 [768, 768], P('mp', ('dp', 'win'))
- grad_table: float32 [169, 24], P(None, 'mp')
- gain_gradient: float32 [768], replicated
- loss: float32 [], replicated
All inputs are finite; a program needn't handle non-finite values.
Results may differ from a plain program's by a relative error of at most 0.01.
Values may be sent and summed in bfloat16 or wider, within the bound.
A program may use at most 64 MiB of HBM per device.

v0:
```python
import functools

import jax
import jax.numpy as jnp
from jax import lax
from jax.sharding import Mesh
from jax.sharding import PartitionSpec as P

HD = 32
WIN_TOK = 49
TABLE = 169
MP = ("mp_0", "mp_1")
DP_WIN_MP = ("dp", "win", "mp_0", "mp_1")


def joined_along(blocks, dim):
    shape = list(blocks.shape[1:])
    shape[dim] *= blocks.shape[0]
    return jnp.moveaxis(blocks, 0, dim).reshape(shape)


def from_everyone(value, axis):
    count = lax.axis_size(axis)
    return lax.all_to_all(
        jnp.broadcast_to(value[None], (count, *value.shape)), axis, 0, 0, tiled=True
    )


def collect(value, axis, dim):
    return joined_along(from_everyone(value, axis), dim)


def split_up(value, dim, count):
    before, after = (value.shape[:dim], value.shape[dim + 1 :])
    return jnp.moveaxis(value.reshape(*before, count, -1, *after), dim, 0)


def sent_and_summed(value, axis, dim):
    count = lax.axis_size(axis)
    blocks = lax.all_to_all(split_up(value, dim, count), axis, 0, 0, tiled=True)
    return jnp.sum(blocks.astype(jnp.float32), axis=0)


def by_axis(value, axes):
    return functools.reduce(lax.psum, axes, value)


def per_device(tokens, target, regions, rel_index, layer_norm_gain, bias_table, w_qkv, w_proj):
    f32 = jnp.float32
    brain_float_sixteen = jnp.bfloat16
    owned_rows = tokens.shape[0]
    channel_count = tokens.shape[1]
    head_cols = w_qkv.shape[1]
    nheads = head_cols // HD
    rows = owned_rows * lax.axis_size(MP)
    windows = rows // WIN_TOK
    everyone = owned_rows * lax.axis_size("dp") * lax.axis_size("win") * lax.axis_size(MP)
    gathered = collect(tokens, MP, 0)
    xfull = gathered.astype(f32)
    mean_value = jnp.mean(xfull, axis=1, keepdims=True)
    centered_input = xfull - mean_value
    var = jnp.mean(centered_input * centered_input, axis=1, keepdims=True)
    inverse_deviation = lax.rsqrt(var + 1e-05)
    normalized_input = centered_input * inverse_deviation
    normed_input = (normalized_input * layer_norm_gain[None, :]).astype(brain_float_sixteen)
    qkv = jnp.einsum("rc,thc->trh", normed_input, w_qkv, preferred_element_type=f32)
    scale = HD ** (-0.5)
    shape4 = (windows, WIN_TOK, nheads, HD)
    query = (qkv[0] * scale).astype(brain_float_sixteen).reshape(shape4)
    keys = qkv[1].astype(brain_float_sixteen).reshape(shape4)
    values = qkv[2].astype(brain_float_sixteen).reshape(shape4)
    onehot = (rel_index.reshape(-1)[:, None] == jnp.arange(TABLE, dtype=jnp.int32)[None, :]).astype(
        f32
    )
    relbias = jnp.dot(onehot, bias_table, precision=lax.Precision.HIGHEST).T.reshape(
        nheads, WIN_TOK, WIN_TOK
    )
    maskv = jnp.where(regions[:, :, None] == regions[:, None, :], 0.0, -100.0).astype(f32)
    scores = jnp.einsum("wqhd,wkhd->whqk", query, keys, preferred_element_type=f32)
    scores = scores + relbias[None] + maskv[:, None]
    top = jnp.max(scores, axis=-1, keepdims=True)
    expo = jnp.exp(scores - top)
    probs = expo / jnp.sum(expo, axis=-1, keepdims=True)
    pb = probs.astype(brain_float_sixteen)
    attn = (
        jnp.einsum("whqk,wkhd->wqhd", pb, values, preferred_element_type=f32)
        .astype(brain_float_sixteen)
        .reshape(rows, head_cols)
    )
    partial_out = jnp.dot(attn, w_proj, preferred_element_type=f32)
    out_share = sent_and_summed(partial_out.astype(jnp.bfloat16), MP, 0)
    error_values = tokens.astype(f32) + out_share - target.astype(f32)
    gb = collect(error_values.astype(brain_float_sixteen), MP, 0)
    dproj = lax.dot_general(attn, gb, (((0,), (0,)), ((), ())), preferred_element_type=f32)
    dattn = lax.dot_general(gb, w_proj, (((1,), (1,)), ((), ())), preferred_element_type=f32)
    dattn = dattn.astype(brain_float_sixteen).reshape(shape4)
    dprob = jnp.einsum("wqhd,wkhd->whqk", dattn, values, preferred_element_type=f32)
    dvalue = jnp.einsum("whqk,wqhd->wkhd", pb, dattn, preferred_element_type=f32)
    dscore = probs * (dprob - jnp.sum(probs * dprob, axis=-1, keepdims=True))
    table_part = jnp.dot(
        jnp.sum(dscore, axis=0).reshape(nheads, -1), onehot, precision=lax.Precision.HIGHEST
    ).T
    dbf = dscore.astype(brain_float_sixteen)
    dquery = jnp.einsum("whqk,wkhd->wqhd", dbf, keys, preferred_element_type=f32) * scale
    dkey = jnp.einsum("whqk,wqhd->wkhd", dbf, query, preferred_element_type=f32)
    dqkv = jnp.stack([dquery, dkey, dvalue]).astype(brain_float_sixteen).reshape(3, rows, head_cols)
    dwqkv = jnp.einsum("trh,rc->thc", dqkv, normed_input, preferred_element_type=f32)
    dxn_part = jnp.einsum("trh,thc->rc", dqkv, w_qkv, preferred_element_type=f32)
    shift_amount = lax.axis_index(MP) * owned_rows
    normalized_input_local = lax.dynamic_slice_in_dim(normalized_input, shift_amount, owned_rows, 0)
    inverse_deviation_local = lax.dynamic_slice_in_dim(
        inverse_deviation, shift_amount, owned_rows, 0
    )
    normed_gradient_local = lax.psum_scatter(
        dxn_part.astype(jnp.bfloat16), MP, scatter_dimension=0, tiled=True
    ).astype(jnp.float32)
    normalized_gradient = normed_gradient_local * layer_norm_gain[None, :]
    gradient_mean_first = jnp.sum(normalized_gradient, axis=1, keepdims=True) / channel_count
    gradient_mean_second = (
        jnp.sum(normalized_gradient * normalized_input_local, axis=1, keepdims=True) / channel_count
    )
    input_gradient = error_values + inverse_deviation_local * (
        normalized_gradient - gradient_mean_first - normalized_input_local * gradient_mean_second
    )
    gain_portion = jnp.sum(normed_gradient_local * normalized_input_local, axis=0)
    halfway = (
        sent_and_summed(dwqkv.astype(jnp.bfloat16), "dp", 2),
        sent_and_summed(dproj.astype(jnp.bfloat16), "dp", 1),
    )
    grad_qkv, grad_proj = (
        sent_and_summed(halfway[0].astype(jnp.bfloat16), "win", 2),
        sent_and_summed(halfway[1].astype(jnp.bfloat16), "win", 1),
    )
    grad_table = by_axis(table_part, ("dp", "win"))
    gain_gradient, total = (
        by_axis(gain_portion, DP_WIN_MP),
        by_axis(jnp.sum(error_values * error_values), DP_WIN_MP),
    )
    shrink_factor = everyone ** (-0.5)
    loss = 0.5 * total / everyone
    return (
        input_gradient,
        grad_qkv * shrink_factor,
        grad_proj * shrink_factor,
        grad_table * shrink_factor,
        gain_gradient * shrink_factor,
        loss,
    )


def solution(mesh):
    split = Mesh(
        mesh.devices.reshape(mesh.shape["dp"], mesh.shape["win"], 4, 2),
        ("dp", "win", "mp_0", "mp_1"),
    )
    return jax.shard_map(
        per_device,
        mesh=split,
        in_specs=(
            P(DP_WIN_MP, None),
            P(DP_WIN_MP, None),
            P(("dp", "win"), None),
            P(),
            P(),
            P(None, MP),
            P(None, MP, None),
            P(MP, None),
        ),
        out_specs=(
            P(DP_WIN_MP, None),
            P(None, MP, ("dp", "win")),
            P(MP, ("dp", "win")),
            P(None, MP),
            P(),
            P(),
        ),
        check_vma=False,
    )
```

profile of v0, /device:TPU:1, one launch (start us, length us, event | category | flops | bytes accessed | tf_op | source)
XLA Modules:
  0.0 260.1 jit_solution(17561513042940202333)
XLA Ops:
  0.6 2.4 broadcast_in_dim.10
  3.0 10.5 %all-to-all-start = ((bf16[8,147,768]{2,1,0:T(8,128)(2,1)}), bf16[8,147,768]{2,1,0:T(8,128)(2,1)S(1)}, u32[]{:S(2)}, u32[]{:S(2)}) async-start(bf16[8,147,768]{2,1,0:T(8,128)(2,1)} %broadcast_in_dim.10), calls=%async_computation | async-start | bytes 3735552 | tf_op jit(solution)/shard_map/all_to_all | solution.py:24
  16.3 21.0 %all-to-all-done = bf16[8,147,768]{2,1,0:T(8,128)(2,1)S(1)} async-done(((bf16[8,147,768]{2,1,0:T(8,128)(2,1)}), bf16[8,147,768]{2,1,0:T(8,128)(2,1)S(1)}, u32[]{:S(2)}, u32[]{:S(2)}) %all-to-all-start) | async-done | bytes 1806368 | tf_op jit(solution)/shard_map/all_to_all | solution.py:24
  38.6 2.2 reshape.139
  40.8 2.4 subtract_multiply_fusion
  47.8 2.5 fusion.55
  57.9 27.5 %all_to_all.35 = bf16[8,147,768]{2,1,0:T(8,128)(2,1)S(1)} all-to-all(bf16[8,147,768]{2,1,0:T(8,128)(2,1)S(1)} %reshape.131), channel_id=1, replica_groups=mesh['dp'=8,'win'=8,'mp_0'=4,'mp_1'=2] {'mp_0','mp_1'}, dimensions={0} | all-to-all | bytes 3612672 | tf_op jit(solution)/shard_map/all_to_all | solution.py:40
  88.1 4.9 %all-to-all-start.2 = ((bf16[8,147,768]{2,1,0:T(8,128)(2,1)}), bf16[8,147,768]{2,1,0:T(8,128)(2,1)}, u32[]{:S(2)}, u32[]{:S(2)}) async-start(bf16[8,147,768]{2,1,0:T(8,128)(2,1)} %broadcast_in_dim.15), calls=%async_computation.2 | async-start | bytes 3735552 | tf_op jit(solution)/shard_map/all_to_all | solution.py:24
  95.7 21.2 %all-to-all-done.2 = bf16[8,147,768]{2,1,0:T(8,128)(2,1)} async-done(((bf16[8,147,768]{2,1,0:T(8,128)(2,1)}), bf16[8,147,768]{2,1,0:T(8,128)(2,1)}, u32[]{:S(2)}, u32[]{:S(2)}) %all-to-all-start.2) | async-done | bytes 1806368 | tf_op jit(solution)/shard_map/all_to_all | solution.py:24
  121.4 2.4 fusion.9
  129.3 2.8 %convolution_convert_fusion.5 = bf16[3,96,768]{2,1,0:T(8,128)(2,1)S(1)} fusion(bf16[3,1176,96]{1,2,0:T(8,128)(2,1)S(1)} %constant_dynamic-update-slice_fusion, f32[1176,768]{1,0:T(8,128)} %copy-done.1, f32[768]{0:T(1024)S(1)} %copy-done.16), kind=kOutput, calls=%fused_computation.25 | convolution fusion | flops 522252288 | bytes 4735488 | tf_op jit(solution)/shard_map/trh,rc->thc/dot_general | solution.py:107
  134.2 5.5 %all-to-all-start.5 = ((bf16[8,96,96]{2,1,0:T(8,128)(2,1)}), bf16[8,96,96]{2,1,0:T(8,128)(2,1)}, u32[]{:S(2)}, u32[]{:S(2)}) async-start(bf16[8,96,96]{2,1,0:T(8,128)(2,1)} %bitcast.75), calls=%async_computation.5 | async-start | bytes 393216 | tf_op jit(solution)/shard_map/all_to_all | solution.py:40
  141.4 17.3 %fusion = bf16[152,768]{1,0:T(8,128)(2,1)S(1)} fusion(bf16[1176,768]{1,0:T(8,128)(2,1)S(1)} %fusion.2), kind=kCustom, calls=%all-reduce-scatter | all-reduce-scatter fusion | flops 933889 | bytes 2041856
  158.8 3.2 %collective-permute-start = (bf16[35,768]{1,0:T(8,128)(2,1)S(1)}, bf16[35,768]{1,0:T(8,128)(2,1)S(1)}, u32[]{:S(2)}, u32[]{:S(2)}) collective-permute-start(bf16[35,768]{1,0:T(8,128)(2,1)S(1)} %slice.17), channel_id=1, source_target_pairs={{0,1},{1,2},{2,3},{3,4},{4,5},{5,6},{6,7},{8,9},{9,10},{10,11},{11... | collective-permute-start | bytes 161288
  168.8 6.8 %all-to-all-start.6 = ((bf16[8,96,12]{1,2,0:T(8,128)(2,1)}), bf16[8,96,12]{1,2,0:T(8,128)(2,1)S(1)}, u32[]{:S(2)}, u32[]{:S(2)}) async-start(bf16[8,96,12]{1,2,0:T(8,128)(2,1)} %bitcast.12), calls=%async_computation.6 | async-start | bytes 65536 | tf_op jit(solution)/shard_map/all_to_all | solution.py:40
  175.6 6.9 %all-to-all-done.6 = bf16[8,96,12]{1,2,0:T(8,128)(2,1)S(1)} async-done(((bf16[8,96,12]{1,2,0:T(8,128)(2,1)}), bf16[8,96,12]{1,2,0:T(8,128)(2,1)S(1)}, u32[]{:S(2)}, u32[]{:S(2)}) %all-to-all-start.6) | async-done | bytes 18464 | tf_op jit(solution)/shard_map/all_to_all | solution.py:40
  182.5 6.8 %all-to-all-start.3 = ((bf16[8,3,96,96]{3,2,1,0:T(8,128)(2,1)}), bf16[8,3,96,96]{3,2,1,0:T(8,128)(2,1)S(1)}, u32[]{:S(2)}, u32[]{:S(2)}) async-start(bf16[8,3,96,96]{3,2,1,0:T(8,128)(2,1)} %bitcast.74), calls=%async_computation.3 | async-start | bytes 1179648 | tf_op jit(solution)/shard_map/all_to_all | solution.py:40
  189.3 2.8 %multiply_reduce_fusion.2 = (f32[]{:T(128)}, f32[147,768]{1,0:T(8,128)}) fusion(bf16[147,768]{1,0:T(8,128)(2,1)S(1)} %copy-done.8, f32[147,768]{1,0:T(8,128)S(1)} %convert_reduce_fusion, bf16[147,768]{1,0:T(8,128)(2,1)S(1)} %copy-done.5, f32[147]{0:T(256)S(1)} %get-tuple-element.31, f32[1176,768]{1,0:T(8,128)} %copy-done.1, s32[]{:T(128)S(6)} %select_n.13, ...), kind=kLoop, calls=%fused_computation.64 | loop fusion | flops 1467647 | bytes 2036976 | tf_op jit(solution)/shard_map/reduce_sum | solution.py:137
  192.1 20.4 %all-reduce.3 = (f32[169,3]{0,1:T(4,128)S(1)}, f32[768]{0:T(1024)S(1)}, f32[]{:T(128)}) all-reduce(f32[169,3]{0,1:T(4,128)S(1)} %fusion.3, f32[768]{0:T(1024)S(1)} %get-tuple-element.6, f32[]{:T(128)} %get-tuple-element.21), channel_id=1, replica_groups=mesh['dp'=8,'win'=8,'mp_0'=4,'mp_1'=2] {'dp'}, use_global_device_ids=true, to_apply=%region_14.15 | all-reduce | flops 1276 | bytes 10208 | tf_op jit(solution)/shard_map/psum | solution.py:45
  212.5 12.3 %all-reduce.2 = (f32[169,3]{0,1:T(4,128)S(1)}, f32[768]{0:T(1024)S(1)}, f32[]{:T(128)}) all-reduce(f32[169,3]{0,1:T(4,128)S(1)} %get-tuple-element.12, f32[768]{0:T(1024)S(1)} %get-tuple-element.13, f32[]{:T(128)} %get-tuple-element.14), channel_id=1, replica_groups=mesh['dp'=8,'win'=8,'mp_0'=4,'mp_1'=2] {'win'}, use_global_device_ids=true, to_apply=%region_15.16 | all-reduce | flops 1276 | bytes 10208 | tf_op jit(solution)/shard_map/psum | solution.py:45
  224.8 7.3 %all-reduce.4 = (f32[768]{0:T(1024)S(1)}, f32[]{:T(128)}) all-reduce(f32[768]{0:T(1024)S(1)} %get-tuple-element.10, f32[]{:T(128)} %get-tuple-element.11), channel_id=1, replica_groups=mesh['dp'=8,'win'=8,'mp_0'=4,'mp_1'=2] {'mp_0'}, use_global_device_ids=true, to_apply=%region_19.20 | all-reduce | flops 769 | bytes 6152 | tf_op jit(solution)/shard_map/psum | solution.py:45
  232.1 12.5 %all-reduce.5 = (f32[768]{0:T(1024)S(1)}, f32[]{:T(128)}) all-reduce(f32[768]{0:T(1024)S(1)} %get-tuple-element.15, f32[]{:T(128)} %get-tuple-element.16), channel_id=1, replica_groups=mesh['dp'=8,'win'=8,'mp_0'=4,'mp_1'=2] {'mp_1'}, use_global_device_ids=true, to_apply=%region_20.21 | all-reduce | flops 769 | bytes 6152 | tf_op jit(solution)/shard_map/psum | solution.py:45
  247.4 3.5 %all-to-all-start.4 = ((bf16[8,3,96,12]{2,3,1,0:T(8,128)(2,1)}), bf16[8,3,96,12]{2,3,1,0:T(8,128)(2,1)S(1)}, u32[]{:S(2)}, u32[]{:S(2)}) async-start(bf16[8,3,96,12]{2,3,1,0:T(8,128)(2,1)} %copy.88), calls=%async_computation.4 | async-start | bytes 196608 | tf_op jit(solution)/shard_map/all_to_all | solution.py:40
  251.5 6.8 %all-to-all-done.4 = bf16[8,3,96,12]{2,3,1,0:T(8,128)(2,1)S(1)} async-done(((bf16[8,3,96,12]{2,3,1,0:T(8,128)(2,1)}), bf16[8,3,96,12]{2,3,1,0:T(8,128)(2,1)S(1)}, u32[]{:S(2)}, u32[]{:S(2)}) %all-to-all-start.4) | async-done | bytes 55328 | tf_op jit(solution)/shard_map/all_to_all | solution.py:40
  (123 shorter events, 44.4 us)
Async XLA Ops:
  0.6 42.6 %copy-start = (bf16[3,96,768]{2,1,0:T(8,128)(2,1)S(1)}, bf16[3,96,768]{2,1,0:T(8,128)(2,1)}, u32[]{:S(2)}) copy-start(bf16[3,96,768]{2,1,0:T(8,128)(2,1)} %param.14) | copy-start | bytes 1327108
  3.0 10.5 %copy-start.20 = (s32[49,49]{1,0:T(8,128)S(1)}, s32[49,49]{1,0:T(8,128)}, u32[]{:S(2)}) copy-start(s32[49,49]{1,0:T(8,128)} %param.11) | copy-start | bytes 28816
  3.0 10.6 %copy-start.24 = (f32[169,3]{0,1:T(4,128)S(1)}, f32[169,3]{0,1:T(4,128)}, u32[]{:S(2)}) copy-start(f32[169,3]{0,1:T(4,128)} %param.13) | copy-start | bytes 6088
  3.0 12.1 %copy-start.19 = (s32[24,49]{1,0:T(8,128)S(1)}, s32[24,49]{1,0:T(8,128)}, u32[]{:S(2)}) copy-start(s32[24,49]{1,0:T(8,128)} %param.10) | copy-start | bytes 14116
  3.0 34.2 %all-to-all-start = ((bf16[8,147,768]{2,1,0:T(8,128)(2,1)}), bf16[8,147,768]{2,1,0:T(8,128)(2,1)S(1)}, u32[]{:S(2)}, u32[]{:S(2)}) async-start(bf16[8,147,768]{2,1,0:T(8,128)(2,1)} %broadcast_in_dim.10), calls=%async_computation | async-start | bytes 3735552 | tf_op jit(solution)/shard_map/all_to_all | solution.py:24
  38.5 2.3 copy-start.14
  40.8 2.4 copy-start.16
  43.3 1.8 copy-start.1
  45.0 2.7 %copy-start.9 = (f32[24,49,49]{1,2,0:T(8,128)S(1)}, f32[24,49,49]{1,2,0:T(8,128)}, u32[]{:S(2)}) copy-start(f32[24,49,49]{1,2,0:T(8,128)} %compare_select_fusion) | copy-start | bytes 691492
  46.3 3.9 %copy-start.2 = (bf16[24,49,3,32]{1,0,3,2:T(8,128)(2,1)}, bf16[24,49,3,32]{1,0,3,2:T(8,128)(2,1)S(1)}, u32[]{:S(2)}) copy-start(bf16[24,49,3,32]{1,0,3,2:T(8,128)(2,1)S(1)} %convert_element_type.93) | copy-start | bytes 677380
  88.1 6.8 %copy-start.15 = (f32[8,147]{1,0:T(8,128)S(1)}, f32[8,147]{1,0:T(8,128)}, u32[]{:S(2)}) copy-start(f32[8,147]{1,0:T(8,128)} %copy-done.14) | copy-start | bytes 14116
  88.1 28.8 %all-to-all-start.2 = ((bf16[8,147,768]{2,1,0:T(8,128)(2,1)}), bf16[8,147,768]{2,1,0:T(8,128)(2,1)}, u32[]{:S(2)}, u32[]{:S(2)}) async-start(bf16[8,147,768]{2,1,0:T(8,128)(2,1)} %broadcast_in_dim.15), calls=%async_computation.2 | async-start | bytes 3735552 | tf_op jit(solution)/shard_map/all_to_all | solution.py:24
  121.3 2.4 copy-start.6
  121.4 2.4 copy-start.13
  121.4 2.4 copy-start.18
  133.3 28.8 %copy-start.22 = (s32[2401]{0:T(1024)S(1)}, s32[2401]{0:T(1024)}, u32[]{:S(2)}) copy-start(s32[2401]{0:T(1024)} %copy-done.21) | copy-start | bytes 28816
  134.2 32.8 %all-to-all-start.5 = ((bf16[8,96,96]{2,1,0:T(8,128)(2,1)}), bf16[8,96,96]{2,1,0:T(8,128)(2,1)}, u32[]{:S(2)}, u32[]{:S(2)}) async-start(bf16[8,96,96]{2,1,0:T(8,128)(2,1)} %bitcast.75), calls=%async_computation.5 | async-start | bytes 393216 | tf_op jit(solution)/shard_map/all_to_all | solution.py:40
  158.8 6.5 %collective-permute-start = (bf16[35,768]{1,0:T(8,128)(2,1)S(1)}, bf16[35,768]{1,0:T(8,128)(2,1)S(1)}, u32[]{:S(2)}, u32[]{:S(2)}) collective-permute-start(bf16[35,768]{1,0:T(8,128)(2,1)S(1)} %slice.17), channel_id=1, source_target_pairs={{0,1},{1,2},{2,3},{3,4},{4,5},{5,6},{6,7},{8,9},{9,10},{10,11},{11... | collective-permute-start | bytes 161288
  164.3 25.0 %copy-start.5 = (bf16[147,768]{1,0:T(8,128)(2,1)S(1)}, bf16[147,768]{1,0:T(8,128)(2,1)}, u32[]{:S(2)}) copy-start(bf16[147,768]{1,0:T(8,128)(2,1)} %param.8) | copy-start | bytes 677380
  164.3 24.9 %copy-start.8 = (bf16[147,768]{1,0:T(8,128)(2,1)S(1)}, bf16[147,768]{1,0:T(8,128)(2,1)}, u32[]{:S(2)}) copy-start(bf16[147,768]{1,0:T(8,128)(2,1)} %param.9) | copy-start | bytes 677380
  164.4 24.9 %copy-start.23 = (f32[147,1]{0,1:T(1,128)S(1)}, f32[147,1]{0,1:T(1,128)}, u32[]{:S(2)}) copy-start(f32[147,1]{0,1:T(1,128)} %constant_dynamic-slice_fusion) | copy-start | bytes 1768
  168.8 13.7 %all-to-all-start.6 = ((bf16[8,96,12]{1,2,0:T(8,128)(2,1)}), bf16[8,96,12]{1,2,0:T(8,128)(2,1)S(1)}, u32[]{:S(2)}, u32[]{:S(2)}) async-start(bf16[8,96,12]{1,2,0:T(8,128)(2,1)} %bitcast.12), calls=%async_computation.6 | async-start | bytes 65536 | tf_op jit(solution)/shard_map/all_to_all | solution.py:40
  182.5 64.0 %all-to-all-start.3 = ((bf16[8,3,96,96]{3,2,1,0:T(8,128)(2,1)}), bf16[8,3,96,96]{3,2,1,0:T(8,128)(2,1)S(1)}, u32[]{:S(2)}, u32[]{:S(2)}) async-start(bf16[8,3,96,96]{3,2,1,0:T(8,128)(2,1)} %bitcast.74), calls=%async_computation.3 | async-start | bytes 1179648 | tf_op jit(solution)/shard_map/all_to_all | solution.py:40
  247.4 10.9 %all-to-all-start.4 = ((bf16[8,3,96,12]{2,3,1,0:T(8,128)(2,1)}), bf16[8,3,96,12]{2,3,1,0:T(8,128)(2,1)S(1)}, u32[]{:S(2)}, u32[]{:S(2)}) async-start(bf16[8,3,96,12]{2,3,1,0:T(8,128)(2,1)} %copy.88), calls=%async_computation.4 | async-start | bytes 196608 | tf_op jit(solution)/shard_map/all_to_all | solution.py:40
  (8 other events, 8.1 us)
where the time goes:
time: 262 us; the launch traced here: 260 us
  blocking collectives  97.4 us (37%)
  waiting for transfers between devices  56 us (21%)
  starting transfers between devices  41.2 us (16%)
  local copies, waits for them, and re-layouts  27.7 us (11%)
  matrix products  20.4 us (8%)
  other arithmetic  13.9 us (5%)
  between operations  3.64 us (1%)
    psum x4, blocking collectives, by_axis(): return functools.reduce(lax.psum, axes, value)  52.6 us
    all_to_all x2, waiting for transfers between devices, from_everyone(): lax.all_to_all(jnp.broadcast_to(value[None], (count, *value.shape)), axis...  42.2 us
    all_to_all x1, blocking collectives, sent_and_summed(): blocks = lax.all_to_all(split_up(value, dim, count), axis, 0, 0, tiled=True)  27.5 us
    all_to_all x4, starting transfers between devices, sent_and_summed(): blocks = lax.all_to_all(split_up(value, dim, count), axis, 0, 0, tiled=True)  22.6 us
    unnamed x1, blocking collectives  17.3 us
    all_to_all x2, starting transfers between devices, from_everyone(): lax.all_to_all(jnp.broadcast_to(value[None], (count, *value.shape)), axis...  15.4 us
    all_to_all x4, waiting for transfers between devices, sent_and_summed(): blocks = lax.all_to_all(split_up(value, dim, count), axis, 0, 0, tiled=True)  13.7 us
  transfers between devices with their start and end apart: 7, of which 4 were waited for; matrix products, arithmetic and copies ran while one was open for 13% of the time, Pallas kernels for 0%

commit v1 on v0

v1 whole, which is shorter than its diff:
```python
import jax
import jax.numpy as jnp
from jax import lax
from jax.experimental import pallas as pl
from jax.experimental.pallas import tpu as pltpu
from jax.sharding import Mesh
from jax.sharding import PartitionSpec as P

C = 768
HD = 32
WIN_TOK = 49
TABLE = 169
ENT = 176
F32 = jnp.float32
BF16 = jnp.bfloat16
MESH = pl.DeviceIdType.MESH
VM = pl.BlockSpec(memory_space=pltpu.VMEM)


def dot(a, b, ca, cb):
    return lax.dot_general(a, b, (((ca,), (cb,)), ((), ())), preferred_element_type=F32)


def onehot_rows(relp, p):
    rows = jnp.concatenate([relp[16 * a + p : 16 * a + p + 1, 0:64] for a in range(4)], axis=1)
    entry = lax.broadcasted_iota(jnp.int32, (ENT, 256), 0)
    return jnp.where(entry == rows, 1.0, 0.0).astype(BF16)


def compute_kernel(
    tok_ref, tgt_ref, reg_ref, rel_ref, gain_ref, w_ref, tab_ref,
    gi_ref, gy_ref, gx_ref, gz_ref, sm_ref,
    pad_s, x_s, t_s, xh_s, xn_s, xt_s, xtp_s, gt_s, ysum_s, err_s, gb_s, dxn_s,
    relp_s, bt_s, bias_s, p_s, q_s, k_s, v_s, at_s, dsum_s,
):
    mp = lax.axis_index("x") * 2 + lax.axis_index("core")
    scale = HD**-0.5
    x_s[...] = jnp.zeros_like(x_s)
    t_s[...] = jnp.zeros_like(t_s)
    pad_s[0:147, :] = tok_ref[...].astype(F32)
    for w in range(3):
        x_s[64 * w : 64 * w + 49, :] = pad_s[49 * w : 49 * w + 49, :]
    pad_s[0:147, :] = tgt_ref[...].astype(F32)
    for w in range(3):
        t_s[64 * w : 64 * w + 49, :] = pad_s[49 * w : 49 * w + 49, :]
    x = x_s[...]
    mean = jnp.sum(x, axis=1, keepdims=True) * (1.0 / C)
    cen = x - mean
    var = jnp.sum(cen * cen, axis=1, keepdims=True) * (1.0 / C)
    inv = lax.rsqrt(var + 1e-05)
    xhat = cen * inv
    xh_s[...] = xhat
    xnf = xhat * gain_ref[...]
    xn_s[...] = xnf.astype(BF16)
    xt = jnp.transpose(xn_s[...].astype(F32))
    xt_s[:, 0:192] = xt.astype(BF16)
    pad2 = xtp_s
    pad2[...] = xt
    for y in range(8):
        blk = jnp.concatenate([pad2[96 * z + 12 * y : 96 * z + 12 * y + 12, :] for z in range(8)], axis=0)
        gt_s[96 * y : 96 * y + 96, :] = blk.astype(BF16)

    relp_s[...] = jnp.full(relp_s.shape, -1, jnp.int32)
    relp_s[0:49, 0:49] = rel_ref[...]
    relp = relp_s[...]
    tab = jnp.concatenate([tab_ref[g, 0:3, 0:ENT] for g in range(8)], axis=0)
    hi = tab.astype(BF16)
    rest = tab - hi.astype(F32)
    mid = rest.astype(BF16)
    low = (rest - mid.astype(F32)).astype(BF16)
    zero8 = jnp.zeros((8, ENT), F32)
    parts = jnp.concatenate(
        [t for one in (hi, mid, low) for t in (one.astype(F32), zero8)], axis=0
    ).astype(BF16)
    for p in range(16):
        got = dot(parts, onehot_rows(relp, p), 1, 0)
        got = got[0:24] + got[32:56] + got[64:88]
        bt_s.at[0][pl.ds(p, 24, stride=16), :] = got[:, 0:128]
        bt_s.at[1][pl.ds(p, 24, stride=16), :] = got[:, 128:256]
    keypad = jnp.where(lax.broadcasted_iota(jnp.int32, (64, 384), 0) < WIN_TOK, 0.0, -1e30)
    for i in range(4):
        turned = [jnp.transpose(bt_s[j, 96 * i : 96 * i + 96, :]) for j in range(2)]
        turned = [t[64 * a : 64 * a + 64] for t in turned for a in range(2)]
        bias_s[i] = jnp.concatenate(turned, axis=1) + keypad

    regs = jnp.concatenate(
        [reg_ref[pl.ds(3 * mp + w, 1), :].astype(F32) for w in range(3)] + [jnp.zeros((5, 49), F32)], axis=0
    )
    regs = jnp.concatenate([regs, jnp.zeros((8, 15), F32)], axis=1)
    lane = lax.broadcasted_iota(jnp.int32, (64, 384), 1)
    query_of = (lane // 96) * 16 + lane % 16
    pick = jnp.where(lax.broadcasted_iota(jnp.int32, (64, 384), 0) == query_of, 1.0, 0.0)
    reg_q = dot(regs, pick, 1, 0)
    eye = jnp.where(
        lax.broadcasted_iota(jnp.int32, (64, 64), 0) == lax.broadcasted_iota(jnp.int32, (64, 64), 1), 1.0, 0.0
    )
    reg_k = dot(eye, regs, 1, 1)

    def shift_mask(w):
        return jnp.where(reg_k[:, w : w + 1] == reg_q[w : w + 1, :], 0.0, -100.0)

    row = lax.broadcasted_iota(jnp.int32, (96, 192), 0)
    col = lax.broadcasted_iota(jnp.int32, (96, 192), 1)
    own = jnp.where(row // 16 == col // 32, 1.0, 0.0)
    own_bf = own.astype(BF16)

    def spread(block):
        return jnp.concatenate(
            [jnp.concatenate([block[16 * a : 16 * a + 16]] * 6, axis=0) * own_bf for a in range(4)], axis=0
        )

    def collapse(big):
        out = []
        for a in range(4):
            part = big[96 * a : 96 * a + 96] * own
            out.append(sum(part[16 * h : 16 * h + 16] for h in range(6)))
        return jnp.concatenate(out, axis=0)

    ysum_s[...] = jnp.zeros_like(ysum_s)

    def forward(i, carry):
        xn = xn_s[...]
        wq = w_ref[i, 0].reshape(192, C)
        wk = w_ref[i, 1].reshape(192, C)
        wv = w_ref[i, 2].reshape(192, C)
        q_s[i] = (dot(xn, wq, 1, 1) * scale).astype(BF16)
        k_s[i] = dot(xn, wk, 1, 1).astype(BF16)
        v_s[i] = dot(xn, wv, 1, 1).astype(BF16)
        for w in range(3):
            rows = slice(64 * w, 64 * w + 64)
            sc = dot(k_s[i, rows, :], spread(q_s[i, rows, :]), 1, 1)
            sc = sc + bias_s[i] + shift_mask(w)
            ex = jnp.exp(sc - jnp.max(sc, axis=0, keepdims=True))
            pr = ex / jnp.sum(ex, axis=0, keepdims=True)
            p_s[i, w] = pr
            at_s[i, rows, :] = collapse(dot(pr.astype(BF16), v_s[i, rows, :], 0, 0)).astype(BF16)
        ysum_s[...] += dot(at_s[i], w_ref[i, 3].reshape(192, C), 1, 0)
        return carry

    lax.fori_loop(0, 4, forward, 0)

    rowid = lax.broadcasted_iota(jnp.int32, (192, C), 0) % 64
    err = jnp.where(rowid < WIN_TOK, x_s[...] + ysum_s[...] - t_s[...], 0.0)
    err_s[...] = err
    gb_s[...] = err.astype(BF16)
    xt_s[:, 192:384] = jnp.transpose(gb_s[...].astype(F32)).astype(BF16)
    dxn_s[...] = jnp.zeros_like(dxn_s)

    def backward(i, carry):
        datt = dot(gb_s[...], w_ref[i, 3].reshape(192, C), 1, 1).astype(BF16)
        dqs, dks, dvs = [], [], []
        total = jnp.zeros((64, 384), F32)
        for w in range(3):
            rows = slice(64 * w, 64 * w + 64)
            da = spread(datt[rows])
            dp = dot(v_s[i, rows, :], da, 1, 1)
            pr = p_s[i, w]
            ds = pr * (dp - jnp.sum(pr * dp, axis=0, keepdims=True))
            total = total + ds
            db = ds.astype(BF16)
            dvs.append(dot(pr.astype(BF16), da, 1, 0))
            dks.append(dot(db, spread(q_s[i, rows, :]), 1, 0))
            dqs.append(collapse(dot(db, k_s[i, rows, :], 0, 0)) * scale)
        turned = [jnp.transpose(total[:, 96 * a : 96 * a + 96]) for a in range(4)]
        here = pl.ds(pl.multiple_of(96 * i, 96), 96)
        dsum_s[0, here, :] = jnp.concatenate(turned[0:2], axis=1)
        dsum_s[1, here, :] = jnp.concatenate(turned[2:4], axis=1)
        dq = jnp.concatenate(dqs, axis=0)
        dk = jnp.concatenate(dks, axis=0)
        dv = jnp.concatenate(dvs, axis=0)
        dqb, dkb, dvb = dq.astype(BF16), dk.astype(BF16), dv.astype(BF16)
        dxn_s[...] += (
            dot(dqb, w_ref[i, 0].reshape(192, C), 1, 0)
            + dot(dkb, w_ref[i, 1].reshape(192, C), 1, 0)
            + dot(dvb, w_ref[i, 2].reshape(192, C), 1, 0)
        )
        lead = jnp.concatenate([dqb[:, 0:128], dvb[:, 0:128]], axis=1)
        low_half = jnp.concatenate([dq[:, 128:192], dk], axis=1).astype(BF16)
        zeros = jnp.zeros((192, 64), F32)
        high_half = jnp.concatenate(
            [
                jnp.concatenate([dv[:, 128:192], jnp.zeros((192, 192), F32)], axis=1),
                jnp.concatenate([zeros, at_s[i].astype(F32)], axis=1),
            ],
            axis=0,
        ).astype(BF16)
        for b in range(8):
            rows = slice(96 * b, 96 * b + 96)
            one = dot(gt_s[rows, :], lead, 1, 0).astype(BF16)
            gy_ref[0, b, i] = one[:, 0:128]
            gy_ref[1, b, i] = one[:, 128:256]
            two = dot(xt_s[rows, 0:192], low_half, 1, 0).astype(BF16)
            gx_ref[0, i, b] = two[:, 0:128]
            gz_ref[0, b, i] = two[:, 128:256]
            three = dot(xt_s[rows, :], high_half, 1, 0).astype(BF16)
            gx_ref[1, i, b] = three[:, 0:128]
            gz_ref[1, b, i] = three[:, 128:256]
        return carry

    lax.fori_loop(0, 4, backward, 0)

    dxn = dxn_s[...]
    xhat = xh_s[...]
    dxh = dxn * gain_ref[...]
    m1 = jnp.sum(dxh, axis=1, keepdims=True) * (1.0 / C)
    m2 = jnp.sum(dxh * xhat, axis=1, keepdims=True) * (1.0 / C)
    out = err_s[...] + inv * (dxh - m1 - xhat * m2)
    for w in range(3):
        gi_ref[49 * w : 49 * w + 49, :] = out[64 * w : 64 * w + 49, :]
    gain = jnp.sum(dxn * xhat, axis=0, keepdims=True)
    sq = err_s[...]
    loss = jnp.sum(sq * sq, axis=0, keepdims=True)
    loss = sum(loss[:, 128 * j : 128 * j + 128] for j in range(6))
    loss = jnp.sum(loss, axis=1, keepdims=True) + jnp.zeros((1, 128), F32)
    tail = jnp.concatenate(
        [gain[:, 128 * j : 128 * j + 128] for j in range(6)] + [loss, jnp.zeros((1, 128), F32)], axis=0
    )

    dtab = jnp.zeros((64, ENT), F32)
    for p in range(16):
        ds = jnp.concatenate([dsum_s.at[j][pl.ds(p, 24, stride=16), :] for j in range(2)], axis=1)
        top = ds.astype(BF16)
        rem = (ds - top.astype(F32)).astype(BF16)
        z8 = jnp.zeros((8, 256), F32)
        both = jnp.concatenate([top.astype(F32), z8, rem.astype(F32), z8], axis=0).astype(BF16)
        dtab = dtab + dot(both, onehot_rows(relp, p), 1, 1)
    dtab = dtab[0:24] + dtab[32:56]
    for g in range(8):
        sm_ref[g] = jnp.zeros((8, 384), F32)
        sm_ref[g, 0:3, 0:ENT] = dtab[3 * g : 3 * g + 3]
        sm_ref[g, :, 256:384] = tail


def compute(tokens, target, regions, rel_index, gain, weights, tables):
    f = lambda *s: pltpu.VMEM(s, F32)
    b = lambda *s: pltpu.VMEM(s, BF16)
    return pl.pallas_call(
        compute_kernel,
        name="window_compute",
        out_shape=(
            jax.ShapeDtypeStruct((147, C), F32),
            jax.ShapeDtypeStruct((2, 8, 4, 96, 128), BF16),
            jax.ShapeDtypeStruct((2, 4, 8, 96, 128), BF16),
            jax.ShapeDtypeStruct((2, 8, 4, 96, 128), BF16),
            jax.ShapeDtypeStruct((8, 8, 384), F32),
        ),
        in_specs=[VM] * 7,
        out_specs=(VM,) * 5,
        scratch_shapes=[
            f(152, C), f(192, C), f(192, C), f(192, C), b(192, C), b(C, 384), f(C, 192), b(C, 192),
            f(192, C), f(192, C), b(192, C), f(192, C),
            pltpu.VMEM((64, 128), jnp.int32), f(2, 384, 128), f(4, 64, 384), f(4, 3, 64, 384),
            b(4, 192, 192), b(4, 192, 192), b(4, 192, 192), b(4, 192, 192), f(2, 384, 128),
        ],
        compiler_params=pltpu.CompilerParams(vmem_limit_bytes=60 * 2**20),
    )(tokens, target, regions, rel_index, gain, weights, tables)


def place():
    return lax.axis_index("dp"), lax.axis_index("win"), lax.axis_index("x"), lax.axis_index("core")


def meet(peers):
    barrier = pltpu.get_barrier_semaphore()
    for peer in peers:
        pl.semaphore_signal(barrier, inc=1, device_id=peer, device_id_type=MESH)
    pl.semaphore_wait(barrier, len(peers))


def mp_peers(z, y, x, c):
    far = [(z, y, lax.rem(x + d, 4), core) for d in (1, 2, 3) for core in (c, 1 - c)]
    return [(z, y, x, 1 - c)] + far


def shift(v, d, n):
    return lax.rem(v + (d % n), n)


def gather_kernel(
    wqkv_ref, wproj_ref, tab_ref, w_ref, t_ref,
    send_x, recv_x, send_y, recv_y, send_z, recv_z, send_c, recv_c, send_t, recv_t, own_sem,
):
    z, y, x, c = place()
    color = lax.rem(y + 2 * z, 4)
    partner = (z, y, x, 1 - c)
    mine = 2 * x + c
    talk = mp_peers(z, y, x, c)
    ys = [(z, shift(y, d, 8), x, c) for d in (1, -1)]
    zs = [(shift(z, d, 8), y, x, c) for d in (1, -1)]
    meet(talk + ys + zs)

    started = []

    def push(src, dst, ssem, rsem, to):
        copy = pltpu.make_async_remote_copy(
            src_ref=src, dst_ref=dst, send_sem=ssem, recv_sem=rsem, device_id=to, device_id_type=MESH
        )
        copy.start()
        started.append(copy)

    def landed(dst, rsem):
        pltpu.make_async_remote_copy(
            src_ref=dst, dst_ref=dst, send_sem=rsem, recv_sem=rsem, device_id=partner, device_id_type=MESH
        ).wait_recv()

    for j, d in enumerate((1, -1)):
        to = (z, y, shift(x, d, 4), c)
        for one in range(4):
            src = wqkv_ref.at[one] if one < 3 else wproj_ref

            @pl.when(color == one)
            def _(src=src, one=one, to=to, j=j):
                pltpu.make_async_remote_copy(
                    src_ref=src, dst_ref=w_ref.at[x, one, c], send_sem=send_x.at[j],
                    recv_sem=recv_x.at[j], device_id=to, device_id_type=MESH,
                ).start()

    for j, to in enumerate(talk):
        push(tab_ref, t_ref.at[mine], send_t.at[j], recv_t.at[j], to)
    for one in range(4):
        src = wqkv_ref.at[one] if one < 3 else wproj_ref
        push(src, w_ref.at[x, one, c], send_c.at[one], recv_c.at[one], partner)
    locals_ = []
    for one in range(4):
        src = wqkv_ref.at[one] if one < 3 else wproj_ref
        local = pltpu.make_async_copy(src, w_ref.at[x, one, c], own_sem.at[one])
        local.start()
        locals_.append(local)
    local = pltpu.make_async_copy(tab_ref, t_ref.at[mine], own_sem.at[4])
    local.start()
    locals_.append(local)

    def half(j):
        return pl.ds(48 * j, 48)

    def hand_on(slot, xs):
        piece = w_ref.at[xs, color, c]
        for j in range(2):
            push(piece, piece, send_y.at[slot, j], recv_y.at[slot, j], ys[j])
        for j in range(2):
            part = w_ref.at[xs, color, c, half(j)]
            push(part, part, send_z.at[slot, j], recv_z.at[slot, j], zs[j])
        push(piece, piece, send_c.at[4 + 5 * slot], recv_c.at[4 + 5 * slot], partner)

    sources = [shift(x, -1, 4), shift(x, 1, 4)]
    for slot in range(2):
        piece = w_ref.at[sources[slot], color, c]
        landed(piece, recv_x.at[slot])
        part = w_ref.at[sources[slot], color, c, half(slot)]
        push(part, part, send_x.at[2 + slot], recv_x.at[2 + slot], (z, y, shift(x, 1 - 2 * slot, 4), c))
        hand_on(slot, sources[slot])
    opposite = shift(x, 2, 4)
    for slot in range(2):
        landed(w_ref.at[opposite, color, c, half(slot)], recv_x.at[2 + slot])
    hand_on(2, opposite)

    sources.append(opposite)
    after = lax.rem(color + 1, 4)
    before = lax.rem(color + 3, 4)
    across = lax.rem(color + 2, 4)
    for slot in range(3):
        xs = sources[slot]
        for j, tint in enumerate((before, after)):
            piece = w_ref.at[xs, tint, c]
            landed(piece, recv_y.at[slot, j])
            at = 5 + 5 * slot + j
            push(piece, piece, send_c.at[at], recv_c.at[at], partner)
        for j in range(2):
            part = w_ref.at[xs, across, c, half(j)]
            landed(part, recv_z.at[slot, j])
            at = 7 + 5 * slot + j
            push(part, part, send_c.at[at], recv_c.at[at], partner)

    other = 1 - c
    for one in range(4):
        landed(w_ref.at[x, one, other], recv_c.at[one])
    for slot in range(3):
        xs = sources[slot]
        landed(w_ref.at[xs, color, other], recv_c.at[4 + 5 * slot])
        landed(w_ref.at[xs, before, other], recv_c.at[5 + 5 * slot])
        landed(w_ref.at[xs, after, other], recv_c.at[6 + 5 * slot])
        for j in range(2):
            landed(w_ref.at[xs, across, other, half(j)], recv_c.at[7 + 5 * slot + j])
    landed(t_ref.at[2 * x + other], recv_t.at[0])
    for d in (1, 2, 3):
        from_x = shift(x, -d, 4)
        landed(t_ref.at[2 * from_x + c], recv_t.at[2 * d - 1])
        landed(t_ref.at[2 * from_x + other], recv_t.at[2 * d])
    for copy in started:
        copy.wait_send()
    for j in range(2):
        pltpu.make_async_remote_copy(
            src_ref=wproj_ref, dst_ref=wproj_ref, send_sem=send_x.at[j], recv_sem=recv_x.at[j],
            device_id=partner, device_id_type=MESH,
        ).wait_send()
    for local in locals_:
        local.wait()


def gather(w_qkv, w_proj, table):
    dma = pltpu.SemaphoreType.DMA
    return pl.pallas_call(
        gather_kernel,
        name="gather_weights",
        out_shape=(
            jax.ShapeDtypeStruct((4, 4, 2, 96, C), BF16),
            jax.ShapeDtypeStruct((8, 8, 256), F32),
        ),
        in_specs=[VM] * 3,
        out_specs=(VM, VM),
        scratch_shapes=[
            dma((4,)), dma((4,)), dma((3, 2)), dma((3, 2)), dma((3, 2)), dma((3, 2)),
            dma((19,)), dma((19,)), dma((7,)), dma((7,)), dma((5,)),
        ],
        compiler_params=pltpu.CompilerParams(
            collective_id=0, has_side_effects=True, vmem_limit_bytes=40 * 2**20
        ),
    )(w_qkv, w_proj, table)


def reduce_kernel(
    gy_ref, gx_ref, gz_ref, sm_ref, out_ref, small_ref,
    ry, rx, rz, cy, cx, cz, s2y, s2x, s2z, flat, a3, b3, r3a, r3b, part_s, sm0, sm1, sm2, ss1, ss2,
    send_d, recv_d, send_r, recv_r, send_2, recv_2, send_3, recv_3, send_s, recv_s, send_f, recv_f,
):
    z, y, x, c = place()
    partner = (z, y, x, 1 - c)
    talk = mp_peers(z, y, x, c)
    line_y = [(z, shift(y, d, 8), x, c) for d in range(1, 8)]
    line_z = [(shift(z, d, 8), y, x, c) for d in range(1, 8)]
    line_x = [(z, y, shift(x, d, 4), c) for d in range(1, 4)]
    meet(talk + line_y + line_z)
    started = []

    def push(src, dst, ssem, rsem, to):
        copy = pltpu.make_async_remote_copy(
            src_ref=src, dst_ref=dst, send_sem=ssem, recv_sem=rsem, device_id=to, device_id_type=MESH
        )
        copy.start()
        started.append(copy)

    def landed(dst, rsem):
        pltpu.make_async_remote_copy(
            src_ref=dst, dst_ref=dst, send_sem=rsem, recv_sem=rsem, device_id=partner, device_id_type=MESH
        ).wait_recv()

    parts = (
        (0, gy_ref, ry, cy, y, 8, 4, lambda d: (z, shift(y, d, 8), x, c)),
        (1, gz_ref, rz, cz, z, 8, 4, lambda d: (shift(z, d, 8), y, x, c)),
        (2, gx_ref, rx, cx, x, 4, 8, lambda d: (z, y, shift(x, d, 4), c)),
    )

    def offsets(n):
        half = n // 2
        return [half] + [sign * d for d in range(half - 1, 0, -1) for sign in (1, -1)] + [0]

    for j, peer in enumerate(talk):
        to = 2 * peer[2] + peer[3]
        push(sm_ref.at[to], sm0.at[j], send_s.at[j], recv_s.at[j], peer)

    for k in range(8):
        for num, g, r, ring, me, n, m, reach in parts:
            if k < n:
                block = shift(me, offsets(n)[k], n)
                push(g.at[1 - c, block], r.at[block], send_d.at[num, k], recv_d.at[num, k], partner)

    def take(part, k):
        num, g, r, ring, me, n, m, reach = part
        block = shift(me, offsets(n)[k], n)
        landed(r.at[block], recv_d.at[num, k])
        for s in range(m):
            r[block, s] = r[block, s] + g[c, block, s]
        return block

    def send_chunk(part, block, sign, step, chunk):
        num, g, r, ring, me, n, m, reach = part
        h = m // 2
        way = 0 if sign == 1 else 1
        push(
            r.at[block, pl.ds(chunk * h, h)], ring.at[way, step - 1, chunk],
            send_r.at[num, way, step - 1, chunk], recv_r.at[num, way, step - 1, chunk], reach(sign),
        )

    def add_chunk(part, block, sign, step, chunk):
        num, g, r, ring, me, n, m, reach = part
        h = m // 2
        way = 0 if sign == 1 else 1
        landed(ring.at[way, step - 1, chunk], recv_r.at[num, way, step - 1, chunk])
        for s in range(h):
            r[block, chunk * h + s] = r[block, chunk * h + s] + ring[way, step - 1, chunk, s]

    for part in parts:
        block = take(part, 0)
        send_chunk(part, block, 1, 1, 0)
        send_chunk(part, block, -1, 1, 1)
    blocks = {}
    for k in range(1, 8):
        for part in parts:
            if k < part[5]:
                blocks[part[0], offsets(part[5])[k]] = take(part, k)

    def level(part, step):
        half = part[5] // 2
        for chunk in range(2):
            for sign in (1, -1):
                block = blocks[part[0], sign * (half + 1 - step)]
                if step > 2 or (chunk == 0) == (sign == 1):
                    add_chunk(part, block, sign, step - 1, chunk)
                send_chunk(part, block, sign, step, chunk)

    def finish(part):
        half = part[5] // 2
        for chunk in range(2):
            for sign in (1, -1):
                add_chunk(part, blocks[part[0], 0], sign, half, chunk)

    for part in parts:
        level(part, 2)
    for j in range(7):
        landed(sm0.at[j], recv_s.at[j])
    ss1[...] = sm_ref[2 * x + c] + sum(sm0[j] for j in range(7))
    for j, to in enumerate(line_y):
        push(ss1, sm1.at[j], send_s.at[7 + j], recv_s.at[7 + j], to)
    finish(parts[2])
    for j, d in enumerate(range(1, 8)):
        push(rx.at[x, shift(z, d, 8)], s2x.at[j], send_2.at[j], recv_2.at[j], line_z[j])
    for part in parts[:2]:
        level(part, 3)
    for part in parts[:2]:
        level(part, 4)
    for j in range(7):
        landed(sm1.at[j], recv_s.at[7 + j])
    ss2[...] = ss1[...] + sum(sm1[j] for j in range(7))
    for j, to in enumerate(line_z):
        push(ss2, sm2.at[j], send_s.at[14 + j], recv_s.at[14 + j], to)
    finish(parts[0])
    for j, d in enumerate(range(1, 4)):
        push(ry.at[y, shift(x, d, 4)], s2y.at[j], send_2.at[7 + j], recv_2.at[7 + j], line_x[j])
    finish(parts[1])
    for j, d in enumerate(range(1, 4)):
        push(rz.at[z, shift(x, d, 4)], s2z.at[j], send_2.at[10 + j], recv_2.at[10 + j], line_x[j])

    a3[...] = jnp.zeros_like(a3)
    b3[...] = jnp.zeros_like(b3)
    total = rx[x, z].astype(F32)
    for j in range(7):
        landed(s2x.at[j], recv_2.at[j])
        total = total + s2x[j].astype(F32)
    flat[0] = total
    for i in range(8):
        b3[i, 0, 0:12, :] = flat[0, 12 * i : 12 * i + 12, :]
    total = ry[y, x].astype(F32)
    for j in range(3):
        landed(s2y.at[j], recv_2.at[7 + j])
        total = total + s2y[j].astype(F32)
    flat[1] = total
    for i in range(8):
        a3[i, 0:12, :] = flat[1, 12 * i : 12 * i + 12, :]
    for j, d in enumerate(range(1, 8)):
        push(a3.at[shift(z, d, 8)], r3a.at[j], send_3.at[j], recv_3.at[j], line_z[j])
    total = rz[z, x].astype(F32)
    for j in range(3):
        landed(s2z.at[j], recv_2.at[10 + j])
        total = total + s2z[j].astype(F32)
    flat[2] = total
    for i in range(8):
        b3[i, 1, 0:12, :] = flat[2, 12 * i : 12 * i + 12, :]
    for j, d in enumerate(range(1, 8)):
        push(b3.at[shift(y, d, 8)], r3b.at[j], send_3.at[7 + j], recv_3.at[7 + j], line_y[j])

    total = ss2[...]
    for j in range(7):
        landed(sm2.at[j], recv_s.at[14 + j])
        total = total + sm2[j]
    small_ref[...] = total
    total = a3[z]
    for j in range(7):
        landed(r3a.at[j], recv_3.at[j])
        total = total + r3a[j]
    part_s[:, 0:128] = total
    total = b3[y]
    for j in range(7):
        landed(r3b.at[j], recv_3.at[7 + j])
        total = total + r3b[j]
    part_s[:, 128:256] = total[0]
    part_s[:, 256:384] = total[1]
    out_ref[c] = part_s[...]
    push(part_s, out_ref.at[c], send_f.at[0], recv_f.at[0], partner)
    landed(out_ref.at[1 - c], recv_f.at[0])
    for copy in started:
        copy.wait_send()


def reduce_all(gy, gx, gz, small):
    dma = pltpu.SemaphoreType.DMA
    b = lambda *s: pltpu.VMEM(s, BF16)
    f = lambda *s: pltpu.VMEM(s, F32)
    return pl.pallas_call(
        reduce_kernel,
        name="reduce_gradients",
        out_shape=(
            jax.ShapeDtypeStruct((2, 16, 384), F32),
            jax.ShapeDtypeStruct((8, 384), F32),
        ),
        in_specs=[VM] * 4,
        out_specs=(VM, VM),
        scratch_shapes=[
            b(8, 4, 96, 128), b(4, 8, 96, 128), b(8, 4, 96, 128),
            b(2, 4, 2, 2, 96, 128), b(2, 2, 2, 4, 96, 128), b(2, 4, 2, 2, 96, 128),
            b(3, 96, 128), b(7, 96, 128), b(3, 96, 128), f(3, 96, 128),
            f(8, 16, 128), f(8, 2, 16, 128), f(7, 16, 128), f(7, 2, 16, 128), f(16, 384),
            f(7, 8, 384), f(7, 8, 384), f(7, 8, 384), f(8, 384), f(8, 384),
            dma((3, 8)), dma((3, 8)), dma((3, 2, 4, 2)), dma((3, 2, 4, 2)), dma((13,)), dma((13,)),
            dma((14,)), dma((14,)), dma((21,)), dma((21,)), dma((1,)), dma((1,)),
        ],
        compiler_params=pltpu.CompilerParams(
            collective_id=1, has_side_effects=True, vmem_limit_bytes=40 * 2**20
        ),
    )(gy, gx, gz, small)


def per_device(tokens, target, regions, rel_index, layer_norm_gain, bias_table, w_qkv, w_proj):
    table = jnp.pad(bias_table.T, ((0, 5), (0, 256 - TABLE)))
    weights, tables = gather(w_qkv, w_proj, table)
    gi, gy, gx, gz, small = compute(
        tokens, target, regions, rel_index, layer_norm_gain.reshape(1, C), weights, tables
    )
    out, small = reduce_all(gy, gx, gz, small)
    count = everyone(tokens)
    shrink = count**-0.5
    rows = jnp.concatenate([out[0, 0:12], out[1, 0:12]], axis=1).reshape(12, 4, 2, 96)
    rows = lax.dynamic_index_in_dim(rows, lax.axis_index("core"), 2, keepdims=False)
    rows = jnp.transpose(rows, (1, 2, 0)) * shrink
    return (
        gi,
        rows[0:3],
        rows[3],
        small[0:3, 0:TABLE].T * shrink,
        small[0:6, 256:384].reshape(C) * shrink,
        small[6, 256] * (0.5 / count),
    )


def everyone(tokens):
    return tokens.shape[0] * lax.axis_size(DP_WIN_MP)


MP = ("x", "core")
DP_WIN_MP = ("dp", "win", "x", "core")


def solution(mesh):
    split = Mesh(
        mesh.devices.reshape(mesh.shape["dp"], mesh.shape["win"], 4, 2), ("dp", "win", "x", "core")
    )
    return jax.shard_map(
        per_device,
        mesh=split,
        in_specs=(
            P(DP_WIN_MP, None), P(DP_WIN_MP, None), P(("dp", "win"), None), P(), P(),
            P(None, MP), P(None, MP, None), P(MP, None),
        ),
        out_specs=(
            P(DP_WIN_MP, None), P(None, MP, ("dp", "win")), P(MP, ("dp", "win")), P(None, MP), P(), P(),
        ),
        check_vma=False,
    )
```

time: 262 us -> 111 us (0.42)
  blocking collectives: 97.4 us -> 0 us
  Pallas kernels: 0 us -> 93.1 us
  waiting for transfers between devices: 56 us -> 0 us
  starting transfers between devices: 41.2 us -> 0 us
  matrix products: 20.4 us -> 0 us
  local copies, waits for them, and re-layouts: 27.7 us -> 13.7 us
  other arithmetic: 13.9 us -> 1.24 us
    pallas_call x0 -> x3, Pallas kernels: none -> 93.1 us  [the longest x1 40.6 us: reduce_all(): pl.pallas_call(reduce_kernel, name='reduce_gradients', out_shape=(jax.Sha...]
    all_to_all x6 -> x0, waiting for transfers between devices: 56 us -> none  [the longest x2 42.2 us: from_everyone(): lax.all_to_all(jnp.broadcast_to(value[None], (count, *value.shape)), axis...]
    psum x4 -> x0, blocking collectives: 52.6 us -> none  [by_axis(): return functools.reduce(lax.psum, axes, value)]
    all_to_all x6 -> x0, starting transfers between devices: 37.9 us -> none  [the longest x4 22.6 us: sent_and_summed(): blocks = lax.all_to_all(split_up(value, dim, count), axis, 0, 0, tiled=True)]
    all_to_all x1 -> x0, blocking collectives: 27.5 us -> none  [sent_and_summed(): blocks = lax.all_to_all(split_up(value, dim, count), axis, 0, 0, tiled=True)]
    dot_general x13 -> x0, matrix products: 17.9 us -> none  [the longest x1 2.81 us: per_device(): jnp.einsum('trh,rc->thc', dqkv, normed_input, preferred_element_type=f32)]
    unnamed x1 -> x0, blocking collectives: 17.3 us -> none
    reduce_sum x10 -> x0, other arithmetic: 7.79 us -> none  [the longest x1 2.75 us: per_device(): jnp.sum(error_values * error_values)]
  transfers between devices with their start and end apart: 7 -> 0, of which waited for: 4 -> 0; matrix products, arithmetic and copies ran while one was open for 13% -> 0% of each run, Pallas kernels for 0% -> 0%
where the time goes in v1:
time: 111 us
  Pallas kernels  93.1 us (84%)
  local copies, waits for them, and re-layouts  13.7 us (12%)
  between operations  2.48 us (2%)
  other arithmetic  1.24 us (1%)
    pallas_call x1, Pallas kernels, reduce_all(): pl.pallas_call(reduce_kernel, name='reduce_gradients', out_shape=(jax.Sha...  40.6 us
    pallas_call x1, Pallas kernels, gather(): pl.pallas_call(gather_kernel, name='gather_weights', out_shape=(jax.Shape...  32.6 us
    pallas_call x1, Pallas kernels, compute(): pl.pallas_call(compute_kernel, name='window_compute', out_shape=(jax.Shap...  20 us
    unnamed x18, local copies, waits for them, and re-layouts  11 us

profile of v1, /device:TPU:1, one launch (start us, length us, event | category | flops | bytes accessed | tf_op | source)
XLA Modules:
  0.0 110.5 jit_solution(12919724023035227689)
XLA Ops:
  0.6 0.7 pad.4.tab_ref
  1.3 0.0 copy-start.4
  1.3 1.0 copy-done.4
  2.3 0.0 copy-start.5
  2.3 0.9 copy-done.5
  3.2 32.6 %gather_weights.1 = (bf16[4,4,2,96,768]{4,3,2,1,0:T(8,128)(2,1)S(1)}, f32[8,8,256]{2,1,0:T(8,128)S(1)}) custom-call(bf16[3,96,768]{2,1,0:T(8,128)(2,1)S(1)} %copy-done.4, bf16[96,768]{1,0:T(8,128)(2,1)S(1)} %copy-done.5, f32[8,256]{1,0:T(8,128)S(1)} %pad.4.tab_ref), custom_call_target="tpu_custom_call" | custom-call | tf_op jit(solution)/shard_map/gather_weights/pallas_call | solution.py:402
  35.8 0.0 copy-start
  35.8 2.1 %copy-done = bf16[4,4,2,96,768]{4,3,2,1,0:T(8,128)(2,1)} copy-done((bf16[4,4,2,96,768]{4,3,2,1,0:T(8,128)(2,1)}, bf16[4,4,2,96,768]{4,3,2,1,0:T(8,128)(2,1)S(1)}, u32[]{:S(2)}) %copy-start) | copy-done | bytes 4718616
  38.0 0.0 copy-start.7
  38.0 0.6 copy-done.7
  38.6 1.3 %reshape.27.gain_ref = f32[1,768]{1,0:T(1,128)} reshape(f32[768]{0:T(1024)} %param.12) | data formatting | bytes 6144 | tf_op jit(solution)/shard_map/reshape | solution.py:626
  39.9 20.0 %window_compute.1 = (f32[147,768]{1,0:T(8,128)}, bf16[2,8,4,96,128]{4,3,2,1,0:T(8,128)(2,1)}, bf16[2,4,8,96,128]{4,3,2,1,0:T(8,128)(2,1)}, bf16[2,8,4,96,128]{4,3,2,1,0:T(8,128)(2,1)}, f32[8,8,384]{2,1,0:T(8,128)}) custom-call(bf16[147,768]{1,0:T(8,128)(2,1)} %tok_ref.1, bf16[147,768]{1,0:T(8,128)(2,1)} %tgt_ref.1, s32[24,49]{1,0:T(8,128)} %reg_ref.1, ...), custom_call_target="tpu_custom_call" | custom-call | tf_op jit(solution)/shard_map/window_compute/pallas_call | solution.py:237
  59.9 1.4 %copy-done.1 = bf16[2,8,4,96,128]{4,3,2,1,0:T(8,128)(2,1)S(1)} copy-done((bf16[2,8,4,96,128]{4,3,2,1,0:T(8,128)(2,1)S(1)}, bf16[2,8,4,96,128]{4,3,2,1,0:T(8,128)(2,1)}, u32[]{:S(2)}) %copy-start.1) | copy-done | bytes 1572888
  61.3 1.4 %copy-done.2 = bf16[2,4,8,96,128]{4,3,2,1,0:T(8,128)(2,1)S(1)} copy-done((bf16[2,4,8,96,128]{4,3,2,1,0:T(8,128)(2,1)S(1)}, bf16[2,4,8,96,128]{4,3,2,1,0:T(8,128)(2,1)}, u32[]{:S(2)}) %copy-start.2) | copy-done | bytes 1572888
  62.7 1.4 %copy-done.3 = bf16[2,8,4,96,128]{4,3,2,1,0:T(8,128)(2,1)S(1)} copy-done((bf16[2,8,4,96,128]{4,3,2,1,0:T(8,128)(2,1)S(1)}, bf16[2,8,4,96,128]{4,3,2,1,0:T(8,128)(2,1)}, u32[]{:S(2)}) %copy-start.3) | copy-done | bytes 1572888
  64.1 0.9 copy-done.6
  65.0 40.6 %reduce_gradients.1 = (f32[2,16,384]{2,1,0:T(8,128)S(1)}, f32[8,384]{1,0:T(8,128)S(1)}) custom-call(bf16[2,8,4,96,128]{4,3,2,1,0:T(8,128)(2,1)S(1)} %copy-done.1, bf16[2,4,8,96,128]{4,3,2,1,0:T(8,128)(2,1)S(1)} %copy-done.2, bf16[2,8,4,96,128]{4,3,2,1,0:T(8,128)(2,1)S(1)} %copy-done.3, f32[8,8,384]{2,1,0:T(8,128)S(1)} %copy-done.6), custom_call_target="tpu_custom_call" | custom-call | tf_op jit(solution)/shard_map/reduce_gradients/pallas_call | solution.py:598
  105.6 0.1 concatenate.8
  105.7 0.1 concatenate.9
  105.8 0.6 copy.16
  106.4 0.6 copy.19
  107.0 0.6 multiply_bitcast_fusion
  107.6 0.6 multiply_bitcast_fusion.1
  108.2 0.5 slice.27
  (7 shorter events, 0.1 us)
Async XLA Ops:
  1.3 1.0 copy-start.4
  2.3 0.9 copy-start.5
  35.8 2.1 %copy-start = (bf16[4,4,2,96,768]{4,3,2,1,0:T(8,128)(2,1)}, bf16[4,4,2,96,768]{4,3,2,1,0:T(8,128)(2,1)S(1)}, u32[]{:S(2)}) copy-start(bf16[4,4,2,96,768]{4,3,2,1,0:T(8,128)(2,1)S(1)} %get-tuple-element.15.w_ref) | copy-start | bytes 14155780
  38.0 0.6 copy-start.7
  59.9 1.4 %copy-start.1 = (bf16[2,8,4,96,128]{4,3,2,1,0:T(8,128)(2,1)S(1)}, bf16[2,8,4,96,128]{4,3,2,1,0:T(8,128)(2,1)}, u32[]{:S(2)}) copy-start(bf16[2,8,4,96,128]{4,3,2,1,0:T(8,128)(2,1)} %get-tuple-element.18.gy_ref) | copy-start | bytes 4718596
  61.3 1.4 %copy-start.2 = (bf16[2,4,8,96,128]{4,3,2,1,0:T(8,128)(2,1)S(1)}, bf16[2,4,8,96,128]{4,3,2,1,0:T(8,128)(2,1)}, u32[]{:S(2)}) copy-start(bf16[2,4,8,96,128]{4,3,2,1,0:T(8,128)(2,1)} %get-tuple-element.19.gx_ref) | copy-start | bytes 4718596
  62.7 1.4 %copy-start.3 = (bf16[2,8,4,96,128]{4,3,2,1,0:T(8,128)(2,1)S(1)}, bf16[2,8,4,96,128]{4,3,2,1,0:T(8,128)(2,1)}, u32[]{:S(2)}) copy-start(bf16[2,8,4,96,128]{4,3,2,1,0:T(8,128)(2,1)} %get-tuple-element.20.gz_ref) | copy-start | bytes 4718596
  64.1 0.9 copy-start.6

commit v2 on v1

--- a/solution.py
+++ b/solution.py
@@ -1,3 +1,5 @@
+import functools
+
 import jax
 import jax.numpy as jnp
 from jax import lax
@@ -50,7 +52,7 @@
     inv = lax.rsqrt(var + 1e-05)
     xhat = cen * inv
     xh_s[...] = xhat
-    xnf = xhat * gain_ref[...]
+    xnf = xhat * gain_ref[...].reshape(1, C)
     xn_s[...] = xnf.astype(BF16)
     xt = jnp.transpose(xn_s[...].astype(F32))
     xt_s[:, 0:192] = xt.astype(BF16)
@@ -201,7 +203,7 @@
 
     dxn = dxn_s[...]
     xhat = xh_s[...]
-    dxh = dxn * gain_ref[...]
+    dxh = dxn * gain_ref[...].reshape(1, C)
     m1 = jnp.sum(dxh, axis=1, keepdims=True) * (1.0 / C)
     m2 = jnp.sum(dxh * xhat, axis=1, keepdims=True) * (1.0 / C)
     out = err_s[...] + inv * (dxh - m1 - xhat * m2)
@@ -231,31 +233,6 @@
         sm_ref[g, :, 256:384] = tail
 
 
-def compute(tokens, target, regions, rel_index, gain, weights, tables):
-    f = lambda *s: pltpu.VMEM(s, F32)
-    b = lambda *s: pltpu.VMEM(s, BF16)
-    return pl.pallas_call(
-        compute_kernel,
-        name="window_compute",
-        out_shape=(
-            jax.ShapeDtypeStruct((147, C), F32),
-            jax.ShapeDtypeStruct((2, 8, 4, 96, 128), BF16),
-            jax.ShapeDtypeStruct((2, 4, 8, 96, 128), BF16),
-            jax.ShapeDtypeStruct((2, 8, 4, 96, 128), BF16),
-            jax.ShapeDtypeStruct((8, 8, 384), F32),
-        ),
-        in_specs=[VM] * 7,
-        out_specs=(VM,) * 5,
-        scratch_shapes=[
-            f(152, C), f(192, C), f(192, C), f(192, C), b(192, C), b(C, 384), f(C, 192), b(C, 192),
-            f(192, C), f(192, C), b(192, C), f(192, C),
-            pltpu.VMEM((64, 128), jnp.int32), f(2, 384, 128), f(4, 64, 384), f(4, 3, 64, 384),
-            b(4, 192, 192), b(4, 192, 192), b(4, 192, 192), b(4, 192, 192), f(2, 384, 128),
-        ],
-        compiler_params=pltpu.CompilerParams(vmem_limit_bytes=60 * 2**20),
-    )(tokens, target, regions, rel_index, gain, weights, tables)
-
-
 def place():
     return lax.axis_index("dp"), lax.axis_index("win"), lax.axis_index("x"), lax.axis_index("core")
 
@@ -287,7 +264,6 @@
     talk = mp_peers(z, y, x, c)
     ys = [(z, shift(y, d, 8), x, c) for d in (1, -1)]
     zs = [(shift(z, d, 8), y, x, c) for d in (1, -1)]
-    meet(talk + ys + zs)
 
     started = []
 
@@ -397,29 +373,8 @@
         local.wait()
 
 
-def gather(w_qkv, w_proj, table):
-    dma = pltpu.SemaphoreType.DMA
-    return pl.pallas_call(
-        gather_kernel,
-        name="gather_weights",
-        out_shape=(
-            jax.ShapeDtypeStruct((4, 4, 2, 96, C), BF16),
-            jax.ShapeDtypeStruct((8, 8, 256), F32),
-        ),
-        in_specs=[VM] * 3,
-        out_specs=(VM, VM),
-        scratch_shapes=[
-            dma((4,)), dma((4,)), dma((3, 2)), dma((3, 2)), dma((3, 2)), dma((3, 2)),
-            dma((19,)), dma((19,)), dma((7,)), dma((7,)), dma((5,)),
-        ],
-        compiler_params=pltpu.CompilerParams(
-            collective_id=0, has_side_effects=True, vmem_limit_bytes=40 * 2**20
-        ),
-    )(w_qkv, w_proj, table)
-
-
 def reduce_kernel(
-    gy_ref, gx_ref, gz_ref, sm_ref, out_ref, small_ref,
+    gy_ref, gx_ref, gz_ref, sm_ref, gq_ref, gp_ref, gtab_ref, ggain_ref, loss_ref, count, out_s,
     ry, rx, rz, cy, cx, cz, s2y, s2x, s2z, flat, a3, b3, r3a, r3b, part_s, sm0, sm1, sm2, ss1, ss2,
     send_d, recv_d, send_r, recv_r, send_2, recv_2, send_3, recv_3, send_s, recv_s, send_f, recv_f,
 ):
@@ -429,7 +384,6 @@
     line_y = [(z, shift(y, d, 8), x, c) for d in range(1, 8)]
     line_z = [(shift(z, d, 8), y, x, c) for d in range(1, 8)]
     line_x = [(z, y, shift(x, d, 4), c) for d in range(1, 4)]
-    meet(talk + line_y + line_z)
     started = []
 
     def push(src, dst, ssem, rsem, to):
@@ -572,7 +526,11 @@
     for j in range(7):
         landed(sm2.at[j], recv_s.at[14 + j])
         total = total + sm2[j]
-    small_ref[...] = total
+    shrink = count**-0.5
+    gtab_ref[...] = total[0:3, 0:TABLE] * shrink
+    for j in range(6):
+        ggain_ref[pl.ds(128 * j, 128)] = total[j : j + 1, 256:384].reshape(128) * shrink
+    loss_ref[...] = total[6:7, 256:384] * (0.5 / count)
     total = a3[z]
     for j in range(7):
         landed(r3a.at[j], recv_3.at[j])
@@ -584,27 +542,65 @@
         total = total + r3b[j]
     part_s[:, 128:256] = total[0]
     part_s[:, 256:384] = total[1]
-    out_ref[c] = part_s[...]
-    push(part_s, out_ref.at[c], send_f.at[0], recv_f.at[0], partner)
-    landed(out_ref.at[1 - c], recv_f.at[0])
+    out_s[c] = part_s[...]
+    push(part_s, out_s.at[c], send_f.at[0], recv_f.at[0], partner)
+    landed(out_s.at[1 - c], recv_f.at[0])
+    for t in range(4):
+        at = 192 * (t % 2)
+        both = out_s[t // 2, 0:12, :] * shrink
+        mine = jnp.where(c == 0, both[:, at : at + 96], both[:, at + 96 : at + 192])
+        if t < 3:
+            gq_ref[t] = mine
+        else:
+            gp_ref[...] = mine
     for copy in started:
         copy.wait_send()
 
 
-def reduce_all(gy, gx, gz, small):
+def whole_kernel(count, *refs):
+    ins, outs, rest = refs[:8], refs[8:14], refs[14:]
+    tok, tgt, reg, rel, gain, table, wqkv, wproj = ins
+    gi, gq, gp, gtab, ggain, loss = outs
+    tab_s, w_s, t_s = rest[:3]
+    gather_s, compute_s, reduce_s = rest[3:14], rest[14:39], rest[39:]
+    z, y, x, c = place()
+    tab_s[...] = jnp.zeros_like(tab_s)
+    tab_s[0:3, 0:TABLE] = table[...]
+    meet(
+        mp_peers(z, y, x, c)
+        + [(z, shift(y, d, 8), x, c) for d in range(1, 8)]
+        + [(shift(z, d, 8), y, x, c) for d in range(1, 8)]
+    )
+    gather_kernel(wqkv, wproj, tab_s, w_s, t_s, *gather_s)
+    gy, gx, gz, sm = compute_s[:4]
+    compute_kernel(tok, tgt, reg, rel, gain, w_s, t_s, gi, gy, gx, gz, sm, *compute_s[4:])
+    reduce_kernel(gy, gx, gz, sm, gq, gp, gtab, ggain, loss, count, *reduce_s)
+
+
+def whole(count, *args):
     dma = pltpu.SemaphoreType.DMA
+    f = lambda *s: pltpu.VMEM(s, F32)
     b = lambda *s: pltpu.VMEM(s, BF16)
-    f = lambda *s: pltpu.VMEM(s, F32)
+    shape = jax.ShapeDtypeStruct
     return pl.pallas_call(
-        reduce_kernel,
-        name="reduce_gradients",
+        functools.partial(whole_kernel, count),
+        name="window_layer",
         out_shape=(
-            jax.ShapeDtypeStruct((2, 16, 384), F32),
-            jax.ShapeDtypeStruct((8, 384), F32),
+            shape((147, C), F32), shape((3, 12, 96), F32), shape((12, 96), F32),
+            shape((3, TABLE), F32), shape((C,), F32), shape((1, 128), F32),
         ),
-        in_specs=[VM] * 4,
-        out_specs=(VM, VM),
+        in_specs=[VM] * 8,
+        out_specs=(VM,) * 6,
         scratch_shapes=[
+            f(8, 256), b(4, 4, 2, 96, C), f(8, 8, 256),
+            dma((4,)), dma((4,)), dma((3, 2)), dma((3, 2)), dma((3, 2)), dma((3, 2)),
+            dma((19,)), dma((19,)), dma((7,)), dma((7,)), dma((5,)),
+            b(2, 8, 4, 96, 128), b(2, 4, 8, 96, 128), b(2, 8, 4, 96, 128), f(8, 8, 384),
+            f(152, C), f(192, C), f(192, C), f(192, C), b(192, C), b(C, 384), f(C, 192), b(C, 192),
+            f(192, C), f(192, C), b(192, C), f(192, C),
+            pltpu.VMEM((64, 128), jnp.int32), f(2, 384, 128), f(4, 64, 384), f(4, 3, 64, 384),
+            b(4, 192, 192), b(4, 192, 192), b(4, 192, 192), b(4, 192, 192), f(2, 384, 128),
+            f(2, 16, 384),
             b(8, 4, 96, 128), b(4, 8, 96, 128), b(8, 4, 96, 128),
             b(2, 4, 2, 2, 96, 128), b(2, 2, 2, 4, 96, 128), b(2, 4, 2, 2, 96, 128),
             b(3, 96, 128), b(7, 96, 128), b(3, 96, 128), f(3, 96, 128),
@@ -614,39 +610,21 @@
             dma((14,)), dma((14,)), dma((21,)), dma((21,)), dma((1,)), dma((1,)),
         ],
         compiler_params=pltpu.CompilerParams(
-            collective_id=1, has_side_effects=True, vmem_limit_bytes=40 * 2**20
+            collective_id=0, has_side_effects=True, vmem_limit_bytes=60 * 2**20
         ),
-    )(gy, gx, gz, small)
-
-
-def per_device(tokens, target, regions, rel_index, layer_norm_gain, bias_table, w_qkv, w_proj):
-    table = jnp.pad(bias_table.T, ((0, 5), (0, 256 - TABLE)))
-    weights, tables = gather(w_qkv, w_proj, table)
-    gi, gy, gx, gz, small = compute(
-        tokens, target, regions, rel_index, layer_norm_gain.reshape(1, C), weights, tables
-    )
-    out, small = reduce_all(gy, gx, gz, small)
-    count = everyone(tokens)
-    shrink = count**-0.5
-    rows = jnp.concatenate([out[0, 0:12], out[1, 0:12]], axis=1).reshape(12, 4, 2, 96)
-    rows = lax.dynamic_index_in_dim(rows, lax.axis_index("core"), 2, keepdims=False)
-    rows = jnp.transpose(rows, (1, 2, 0)) * shrink
-    return (
-        gi,
-        rows[0:3],
-        rows[3],
-        small[0:3, 0:TABLE].T * shrink,
-        small[0:6, 256:384].reshape(C) * shrink,
-        small[6, 256] * (0.5 / count),
-    )
-
-
-def everyone(tokens):
-    return tokens.shape[0] * lax.axis_size(DP_WIN_MP)
+    )(*args)
 
 
 MP = ("x", "core")
 DP_WIN_MP = ("dp", "win", "x", "core")
+
+
+def per_device(tokens, target, regions, rel_index, layer_norm_gain, bias_table, w_qkv, w_proj):
+    count = tokens.shape[0] * lax.axis_size(DP_WIN_MP)
+    gi, gq, gp, gtab, ggain, loss = whole(
+        count, tokens, target, regions, rel_index, layer_norm_gain, bias_table.T, w_qkv, w_proj
+    )
+    return gi, jnp.transpose(gq, (0, 2, 1)), gp.T, gtab.T, ggain, loss[0, 0]
 
 
 def solution(mesh):

time: 111 us -> 94.1 us (0.85)
  local copies, waits for them, and re-layouts: 13.7 us -> 4.49 us
  Pallas kernels: 93.1 us -> 87.5 us
  other arithmetic: 1.24 us -> 0 us
    unnamed x18 -> x15, local copies, waits for them, and re-layouts: 11 us -> 4.49 us
    pallas_call x3 -> x1, Pallas kernels: 93.1 us -> 87.5 us  [whole(): pl.pallas_call(functools.partial(whole_kernel, count), name='window_layer...]
    reshape x1 -> x0, local copies, waits for them, and re-layouts: 1.27 us -> none  [per_device(): layer_norm_gain.reshape(1, C)]
    mul x3 -> x0, other arithmetic: 1.24 us -> none  [the longest x1 0.59 us: per_device(): small[0:6, 256:384].reshape(C) * shrink]
where the time goes in v2:
time: 94.1 us; the launch traced here: 93.8 us
  Pallas kernels  87.5 us (93%)
  local copies, waits for them, and re-layouts  4.49 us (5%)
  between operations  1.82 us (2%)
    pallas_call x1, Pallas kernels, whole(): pl.pallas_call(functools.partial(whole_kernel, count), name='window_layer...  87.5 us
    unnamed x15, local copies, waits for them, and re-layouts  4.49 us

profile of v2, /device:TPU:1, one launch (start us, length us, event | category | flops | bytes accessed | tf_op | source)
XLA Modules:
  0.0 93.8 jit_solution(6920486210186530944)
XLA Ops:
  0.6 87.5 %window_layer.1 = (f32[147,768]{1,0:T(8,128)}, f32[3,12,96]{2,1,0:T(8,128)}, f32[12,96]{1,0:T(8,128)}, f32[3,169]{1,0:T(4,128)}, f32[768]{0:T(1024)}, /*index=5*/f32[1,128]{1,0:T(1,128)}) custom-call(bf16[147,768]{1,0:T(8,128)(2,1)} %refs_0_.1, bf16[147,768]{1,0:T(8,128)(2,1)} %refs_1_.1, s32[24,49]{1,0:T(8,128)} %refs_2_.1, s32[49,49]{1,0:T(8,128)} %refs_3_.1, ...), custom_call_target="tpu_custom_call" | custom-call | tf_op jit(solution)/shard_map/window_layer/pallas_call | solution.py:585
  88.2 0.0 copy-start
  88.2 1.8 %copy.20 = f32[147,768]{1,0:T(8,128)} copy(f32[147,768]{1,0:T(8,128)} %get-tuple-element.24) | data formatting | bytes 903168
  90.0 0.0 copy-done
  90.0 0.0 copy-start.1
  90.0 0.6 copy.21
  90.6 0.1 copy-done.1
  90.7 0.0 copy-start.3
  90.7 0.6 copy.22
  91.3 0.1 copy-done.3
  91.4 0.0 copy-start.2
  91.4 0.6 copy.23
  92.0 0.1 copy-done.2
  92.1 0.0 copy-start.4
  92.1 0.6 copy.24
  92.7 0.0 copy-done.4
Async XLA Ops:
  88.2 1.8 %copy-start = (f32[3,12,96]{2,1,0:T(8,128)S(1)}, f32[3,12,96]{2,1,0:T(8,128)}, u32[]{:S(2)}) copy-start(f32[3,12,96]{2,1,0:T(8,128)} %get-tuple-element.13) | copy-start | bytes 41476
  90.0 0.7 copy-start.1
  90.7 0.7 copy-start.3
  91.4 0.7 copy-start.2
  92.1 0.6 copy-start.4

commit v3 on v0

v3 whole, which is shorter than its diff:
```python
import functools

import jax
import jax.numpy as jnp
from jax import lax
from jax.experimental import pallas as pl
from jax.experimental.pallas import tpu as pltpu
from jax.sharding import Mesh
from jax.sharding import PartitionSpec as P

C = 768
HD = 32
WIN_TOK = 49
TABLE = 169
ENT = 176
F32 = jnp.float32
BF16 = jnp.bfloat16
MESH = pl.DeviceIdType.MESH
VM = pl.BlockSpec(memory_space=pltpu.VMEM)
MP = ("x", "core")
DP_WIN_MP = ("dp", "win", "x", "core")
BIG = (0, C // 2)


def dot(a, b, ca, cb):
    return lax.dot_general(a, b, (((ca,), (cb,)), ((), ())), preferred_element_type=F32)


def onehot_rows(relp, p):
    rows = jnp.concatenate([relp[16 * a + p : 16 * a + p + 1, 0:64] for a in range(4)], axis=1)
    entry = lax.broadcasted_iota(jnp.int32, (ENT, 256), 0)
    return jnp.where(entry == rows, 1.0, 0.0).astype(BF16)


def shift(v, d, n):
    return lax.rem(v + (d % n), n)


def whole_kernel(count, *refs):
    (
        tok_hbm, tgt_hbm, reg_hbm, rel_hbm, gain_hbm, table_hbm, wqkv_hbm, wproj_hbm,
        gi_ref, gq_ref, gp_ref, gtab_ref, ggain_ref, loss_ref,
        tok_ref, tgt_ref, reg_ref, rel_ref, gain_ref, table_ref, tab_s, w_ref, t_ref,
        send_x, recv_x, send_o, recv_o, send_n, recv_n, send_c, recv_c, send_t, recv_t, own_sem,
        pad_s, x_s, t_s, xh_s, xn_s, xt_s, xtf_s, xtp_s, ysum_s, err_s, gb_s, dxn_s,
        relp_s, bt_s, bias_s, p_s, q_s, k_s, v_s, at_s, dsum_s, sm_ref,
        gy_s, gz_s, gx_s, ry, rz, rx, cy, cz, dy, dz, cxf,
        s2y, s2z, s2x, flat, a3, b3, r3a, r3b, part_s, sm0, sm1, sm2, ss1, ss2,
        send_d, recv_d, send_r, recv_r, send_v, recv_v, send_rx, recv_rx,
        send_2, recv_2, send_3, recv_3, send_s, recv_s,
    ) = refs
    z, y, x, c = (lax.axis_index(name) for name in DP_WIN_MP)
    mp = 2 * x + c
    scale = HD**-0.5
    shrink = count**-0.5
    partner = (z, y, x, 1 - c)
    talk = [partner] + [(z, y, shift(x, d, 4), core) for d in (1, 2, 3) for core in (c, 1 - c)]
    line_y = [(z, shift(y, d, 8), x, c) for d in range(1, 8)]
    line_z = [(shift(z, d, 8), y, x, c) for d in range(1, 8)]
    line_x = [(z, y, shift(x, d, 4), c) for d in range(1, 4)]
    started = []

    def push(src, dst, ssem, rsem, to):
        copy = pltpu.make_async_remote_copy(
            src_ref=src, dst_ref=dst, send_sem=ssem, recv_sem=rsem, device_id=to, device_id_type=MESH
        )
        copy.start()
        started.append(copy)

    def landed(dst, rsem):
        pltpu.make_async_remote_copy(
            src_ref=dst, dst_ref=dst, send_sem=rsem, recv_sem=rsem, device_id=partner, device_id_type=MESH
        ).wait_recv()

    barrier = pltpu.get_barrier_semaphore()
    peers = talk + line_y + line_z
    peers += [to[:3] + (1 - c,) for to in line_y + line_z]
    for peer in peers:
        pl.semaphore_signal(barrier, inc=1, device_id=peer, device_id_type=MESH)

    load = [
        pltpu.make_async_copy(src, dst, own_sem.at[k])
        for k, (src, dst) in enumerate(
            (
                (tok_hbm, tok_ref), (wqkv_hbm.at[0], w_ref.at[x, 0, c]), (wqkv_hbm.at[1], w_ref.at[x, 1, c]),
                (wqkv_hbm.at[2], w_ref.at[x, 2, c]), (wproj_hbm, w_ref.at[x, 3, c]), (table_hbm, table_ref),
                (gain_hbm, gain_ref), (tgt_hbm, tgt_ref), (rel_hbm, rel_ref), (reg_hbm, reg_ref),
            )
        )
    ]
    for one in load:
        one.start()
    tab_s[...] = jnp.zeros_like(tab_s)
    load[5].wait()
    tab_s[0:3, 0:TABLE] = table_ref[...]
    t_ref[mp] = tab_s[...]
    load[0].wait()
    load[6].wait()
    load[7].wait()
    x_s[...] = jnp.zeros_like(x_s)
    t_s[...] = jnp.zeros_like(t_s)
    pad_s[0:147, :] = tok_ref[...].astype(F32)
    for w in range(3):
        x_s[64 * w : 64 * w + 49, :] = pad_s[49 * w : 49 * w + 49, :]
    pad_s[0:147, :] = tgt_ref[...].astype(F32)
    for w in range(3):
        t_s[64 * w : 64 * w + 49, :] = pad_s[49 * w : 49 * w + 49, :]
    xx = x_s[...]
    mean = jnp.sum(xx, axis=1, keepdims=True) * (1.0 / C)
    cen = xx - mean
    var = jnp.sum(cen * cen, axis=1, keepdims=True) * (1.0 / C)
    inv = lax.rsqrt(var + 1e-05)
    xh_s[...] = cen * inv
    xn_s[...] = (xh_s[...] * gain_ref[...].reshape(1, C)).astype(BF16)

    pl.semaphore_wait(barrier, len(peers))

    colors = (lax.rem(y + 2 * z, 4), lax.rem(z + 2 * y, 4))
    near_y = [(z, shift(y, d, 8), x, c) for d in (1, -1)]
    near_z = [(shift(z, d, 8), y, x, c) for d in (1, -1)]
    strong = (near_y, near_z)
    weak = (near_z, near_y)

    def rows_of(m):
        return pl.ds(48 * m, 48)

    def piece(xs, tint, core, m):
        return w_ref.at[xs, tint, core, rows_of(m)]

    def lanes(xs, tint, core, m, j):
        return w_ref.at[xs, tint, core, rows_of(m), pl.ds(BIG[j], C // 2)]

    for k in range(1, 5):
        load[k].wait()
    for m in range(2):
        for j, d in enumerate((1, -1)):
            there = piece(x, colors[m], c, m)
            push(there, there, send_x.at[m, j], recv_x.at[m, j], (z, y, shift(x, d, 4), c))
        if m == 0:
            for j, to in enumerate(talk):
                push(tab_s, t_ref.at[mp], send_t.at[j], recv_t.at[j], to)
    for one in range(4):
        there = w_ref.at[x, one, c]
        push(there, there, send_c.at[one], recv_c.at[one], partner)
    load[8].wait()
    load[9].wait()

    xt = jnp.transpose(xn_s[...].astype(F32))
    xt_s[:, 0:192] = xt.astype(BF16)
    xtf_s[...] = xt
    for b in range(8):
        block = jnp.concatenate([xtf_s[96 * k + 12 * b : 96 * k + 12 * b + 12, :] for k in range(8)], axis=0)
        xtp_s[96 * b : 96 * b + 96, :] = block.astype(BF16)
    relp_s[...] = jnp.full(relp_s.shape, -1, jnp.int32)
    relp_s[0:49, 0:49] = rel_ref[...]
    relp = relp_s[...]
    regs = jnp.concatenate(
        [reg_ref[pl.ds(3 * mp + w, 1), :].astype(F32) for w in range(3)] + [jnp.zeros((5, 49), F32)], axis=0
    )
    regs = jnp.concatenate([regs, jnp.zeros((8, 15), F32)], axis=1)
    lane = lax.broadcasted_iota(jnp.int32, (64, 384), 1)
    query_of = (lane // 96) * 16 + lane % 16
    pick = jnp.where(lax.broadcasted_iota(jnp.int32, (64, 384), 0) == query_of, 1.0, 0.0)
    reg_q = dot(regs, pick, 1, 0)
    eye = jnp.where(
        lax.broadcasted_iota(jnp.int32, (64, 64), 0) == lax.broadcasted_iota(jnp.int32, (64, 64), 1), 1.0, 0.0
    )
    reg_k = dot(eye, regs, 1, 1)
    row = lax.broadcasted_iota(jnp.int32, (96, 192), 0)
    col = lax.broadcasted_iota(jnp.int32, (96, 192), 1)
    own = jnp.where(row // 16 == col // 32, 1.0, 0.0)
    own_bf = own.astype(BF16)

    left, right, opposite = shift(x, -1, 4), shift(x, 1, 4), shift(x, 2, 4)
    sources = (left, right, opposite)

    def hand_on(slot, m):
        xs = sources[slot]
        tint = colors[m]
        for j in range(2):
            push(piece(xs, tint, c, m), piece(xs, tint, c, m),
                 send_n.at[slot, m, j], recv_n.at[slot, m, j], strong[m][j])
        for j in range(2):
            push(lanes(xs, tint, c, m, j), lanes(xs, tint, c, m, j),
                 send_n.at[slot, m, 2 + j], recv_n.at[slot, m, 2 + j], weak[m][j])
        push(piece(xs, tint, c, m), piece(xs, tint, c, m),
             send_c.at[4 + 10 * slot + 5 * m], recv_c.at[4 + 10 * slot + 5 * m], partner)

    for m in range(2):
        for slot in range(2):
            landed(piece(sources[slot], colors[m], c, m), recv_x.at[m, slot])
            if slot == m:
                there = piece(sources[slot], colors[m], c, m)
                push(there, there, send_o.at[m], recv_o.at[m], (z, y, shift(x, 1 - 2 * slot, 4), c))
            hand_on(slot, m)

    landed(t_ref.at[2 * x + 1 - c], recv_t.at[0])
    for d in (1, 2, 3):
        landed(t_ref.at[2 * shift(x, -d, 4) + c], recv_t.at[2 * d - 1])
        landed(t_ref.at[2 * shift(x, -d, 4) + 1 - c], recv_t.at[2 * d])
    tab = jnp.concatenate([t_ref[g, 0:3, 0:ENT] for g in range(8)], axis=0)
    hi = tab.astype(BF16)
    rest = tab - hi.astype(F32)
    mid = rest.astype(BF16)
    low = (rest - mid.astype(F32)).astype(BF16)
    zero8 = jnp.zeros((8, ENT), F32)
    parts = jnp.concatenate(
        [t for one in (hi, mid, low) for t in (one.astype(F32), zero8)], axis=0
    ).astype(BF16)
    for p in range(16):
        got = dot(parts, onehot_rows(relp, p), 1, 0)
        got = got[0:24] + got[32:56] + got[64:88]
        bt_s.at[0][pl.ds(p, 24, stride=16), :] = got[:, 0:128]
        bt_s.at[1][pl.ds(p, 24, stride=16), :] = got[:, 128:256]
    keypad = jnp.where(lax.broadcasted_iota(jnp.int32, (64, 384), 0) < WIN_TOK, 0.0, -1e30)
    for i in range(4):
        turned = [jnp.transpose(bt_s[j, 96 * i : 96 * i + 96, :]) for j in range(2)]
        turned = [t[64 * a : 64 * a + 64] for t in turned for a in range(2)]
        bias_s[i] = jnp.concatenate(turned, axis=1) + keypad

    def shift_mask(w):
        return jnp.where(reg_k[:, w : w + 1] == reg_q[w : w + 1, :], 0.0, -100.0)

    def spread(block):
        return jnp.concatenate(
            [jnp.concatenate([block[16 * a : 16 * a + 16]] * 6, axis=0) * own_bf for a in range(4)], axis=0
        )

    def collapse(big):
        out = []
        for a in range(4):
            part = big[96 * a : 96 * a + 96] * own
            out.append(sum(part[16 * h : 16 * h + 16] for h in range(6)))
        return jnp.concatenate(out, axis=0)

    def weight(xs, t):
        return w_ref[xs, t].reshape(192, C)

    def forward(i, xs, first):
        xn = xn_s[...]
        q_s[i] = (dot(xn, weight(xs, 0), 1, 1) * scale).astype(BF16)
        k_s[i] = dot(xn, weight(xs, 1), 1, 1).astype(BF16)
        v_s[i] = dot(xn, weight(xs, 2), 1, 1).astype(BF16)
        for w in range(3):
            rows = slice(64 * w, 64 * w + 64)
            sc = dot(k_s[i, rows, :], spread(q_s[i, rows, :]), 1, 1)
            sc = sc + bias_s[xs] + shift_mask(w)
            ex = jnp.exp(sc - jnp.max(sc, axis=0, keepdims=True))
            pr = ex / jnp.sum(ex, axis=0, keepdims=True)
            p_s[i, w] = pr
            at_s[i, rows, :] = collapse(dot(pr.astype(BF16), v_s[i, rows, :], 0, 0)).astype(BF16)
        part = dot(at_s[i], weight(xs, 3), 1, 0)
        ysum_s[...] = part if first else ysum_s[...] + part

    order = (opposite, right, left, x)

    def near_tints(m):
        return [lax.rem(colors[m] + d, 4) for d in (3, 1)], lax.rem(colors[m] + 2, 4)

    def hand_over(slot):
        xs = sources[slot]
        for m in range(2):
            tints, across = near_tints(m)
            for j in range(2):
                there = piece(xs, tints[j], c, m)
                landed(there, recv_n.at[slot, m, j])
                at = 5 + 10 * slot + 5 * m + j
                push(there, there, send_c.at[at], recv_c.at[at], partner)
            for j in range(2):
                there = lanes(xs, across, c, m, j)
                landed(there, recv_n.at[slot, m, 2 + j])
                at = 7 + 10 * slot + 5 * m + j
                push(there, there, send_c.at[at], recv_c.at[at], partner)

    def whole_slot(slot):
        xs = sources[slot]
        for m in range(2):
            tints, across = near_tints(m)
            at = 4 + 10 * slot + 5 * m
            landed(piece(xs, colors[m], 1 - c, m), recv_c.at[at])
            for j in range(2):
                landed(piece(xs, tints[j], 1 - c, m), recv_c.at[at + 1 + j])
                landed(lanes(xs, across, 1 - c, m, j), recv_c.at[at + 3 + j])

    for m in range(2):
        landed(piece(opposite, colors[m], c, m), recv_o.at[m])
        hand_on(2, m)
    for one in range(4):
        landed(w_ref.at[x, one, 1 - c], recv_c.at[one])
    forward(3, x, True)
    hand_over(0)
    hand_over(1)
    whole_slot(0)
    forward(2, left, False)
    hand_over(2)
    whole_slot(1)
    forward(1, right, False)
    whole_slot(2)
    forward(0, opposite, False)

    rowid = lax.broadcasted_iota(jnp.int32, (192, C), 0) % 64
    err = jnp.where(rowid < WIN_TOK, x_s[...] + ysum_s[...] - t_s[...], 0.0)
    err_s[...] = err
    gb_s[...] = err.astype(BF16)
    xt_s[:, 192:384] = jnp.transpose(err).astype(BF16)

    def backward(i, first):
        xs = order[i]
        datt = dot(gb_s[...], weight(xs, 3), 1, 1).astype(BF16)
        dqs, dks, dvs = [], [], []
        total = jnp.zeros((64, 384), F32)
        for w in range(3):
            rows = slice(64 * w, 64 * w + 64)
            da = spread(datt[rows])
            dp = dot(v_s[i, rows, :], da, 1, 1)
            pr = p_s[i, w]
            ds = pr * (dp - jnp.sum(pr * dp, axis=0, keepdims=True))
            total = total + ds
            db = ds.astype(BF16)
            dvs.append(dot(pr.astype(BF16), da, 1, 0))
            dks.append(dot(db, spread(q_s[i, rows, :]), 1, 0))
            dqs.append(collapse(dot(db, k_s[i, rows, :], 0, 0)) * scale)
        turned = [jnp.transpose(total[:, 96 * a : 96 * a + 96]) for a in range(4)]
        here = pl.ds(pl.multiple_of(96 * xs, 96), 96)
        dsum_s[0, here, :] = jnp.concatenate(turned[0:2], axis=1)
        dsum_s[1, here, :] = jnp.concatenate(turned[2:4], axis=1)
        dq = jnp.concatenate(dqs, axis=0)
        dk = jnp.concatenate(dks, axis=0)
        dv = jnp.concatenate(dvs, axis=0)
        dqb, dkb, dvb = dq.astype(BF16), dk.astype(BF16), dv.astype(BF16)
        lead = jnp.concatenate([dqb[:, 0:128], dvb[:, 0:128]], axis=1)
        low_half = jnp.concatenate([dq[:, 128:192], dk], axis=1).astype(BF16)
        zeros = jnp.zeros((192, 64), F32)
        high_half = jnp.concatenate(
            [
                jnp.concatenate([dv[:, 128:192], jnp.zeros((192, 192), F32)], axis=1),
                jnp.concatenate([zeros, at_s[i].astype(F32)], axis=1),
            ],
            axis=0,
        ).astype(BF16)
        for b in range(8):
            rows = slice(96 * b, 96 * b + 96)
            one = dot(xtp_s[rows, :], lead, 1, 0).astype(BF16)
            gy_s[0, i, b] = one[:, 0:128]
            gy_s[1, i, b] = one[:, 128:256]
            two = dot(xt_s[rows, 0:192], low_half, 1, 0).astype(BF16)
            gx_s[0, i, b] = two[:, 0:128]
            gz_s[0, i, b] = two[:, 128:256]
            three = dot(xt_s[rows, :], high_half, 1, 0).astype(BF16)
            gx_s[1, i, b] = three[:, 0:128]
            gz_s[1, i, b] = three[:, 128:256]
        for num, (g, r) in enumerate(((gy_s, ry), (gz_s, rz), (gx_s, rx))):
            push(g.at[1 - c, i], r.at[i], send_d.at[num, i], recv_d.at[num, i], partner)
        part = (
            dot(dqb, weight(xs, 0), 1, 0) + dot(dkb, weight(xs, 1), 1, 0) + dot(dvb, weight(xs, 2), 1, 0)
        )
        dxn_s[...] = part if first else dxn_s[...] + part

    direct = (dy, dz)
    rings = (
        (0, gy_s, ry, cy, y, lambda d: (z, shift(y, d, 8), x, c)),
        (1, gz_s, rz, cz, z, lambda d: (shift(z, d, 8), y, x, c)),
    )

    def take(i):
        for num, g, r, ring, me, reach in rings:
            landed(r.at[i], recv_d.at[num, i])
            for b in range(8):
                r[i, b] = r[i, b] + g[c, i, b]
            if i < 2:
                far = shift(me, 4, 8)
                for way, sign in enumerate((1, -1)):
                    push(r.at[i, far, rows_of(way)], ring.at[way, 0, i, rows_of(way)],
                         send_r.at[num, way, 0, i], recv_r.at[num, way, 0, i], reach(sign))
            else:
                for d in (4, 3, 5, 2, 6, 1, 7):
                    push(r.at[i, shift(me, d, 8)], direct[num].at[i - 2, d - 1],
                         send_v.at[num, i - 2, d - 1], recv_v.at[num, i - 2, d - 1], reach(d))
        landed(rx.at[i], recv_d.at[2, i])
        for b in range(8):
            rx[i, b] = rx[i, b] + gx_s[c, i, b]
        if i < 3:
            push(rx.at[i], cxf.at[i], send_rx.at[i], recv_rx.at[i], (z, y, order[i], c))

    def step(i, s):
        for num, g, r, ring, me, reach in rings:
            for way, sign in enumerate((1, -1)):
                block = shift(me, sign * (5 - s), 8)
                if s == 2:
                    landed(ring.at[way, 0, i, rows_of(way)], recv_r.at[num, way, 0, i])
                    cut = slice(48 * way, 48 * way + 48)
                    r[i, block, cut, :] = r[i, block, cut, :] + ring[way, 0, i, cut, :]
                else:
                    landed(ring.at[way, s - 2, i], recv_r.at[num, way, s - 2, i])
                    r[i, block] = r[i, block] + ring[way, s - 2, i]
                push(r.at[i, block], ring.at[way, s - 1, i],
                     send_r.at[num, way, s - 1, i], recv_r.at[num, way, s - 1, i], reach(sign))

    def finish(num, i):
        num, g, r, ring, me, reach = rings[num]
        if i < 2:
            for way in range(2):
                landed(ring.at[way, 3, i], recv_r.at[num, way, 3, i])
            total = r[i, me].astype(F32) + ring[0, 3, i].astype(F32) + ring[1, 3, i].astype(F32)
        else:
            total = r[i, me].astype(F32)
            for d in (1, 7, 2, 6, 3, 5, 4):
                landed(direct[num].at[i - 2, d - 1], recv_v.at[num, i - 2, d - 1])
                total = total + direct[num][i - 2, d - 1].astype(F32)
        r[i, me] = total.astype(BF16)
        buf = (s2y, s2z)[num]
        if i < 3:
            to = (z, y, order[i], c)
            push(r.at[i, me], buf.at[i], send_2.at[num, i], recv_2.at[num, i], to)

    backward(0, True)
    backward(1, False)
    take(0)
    backward(2, False)
    take(1)
    step(0, 2)
    backward(3, False)
    take(2)
    step(1, 2)
    step(0, 3)

    dxn = dxn_s[...]
    xhat = xh_s[...]
    dxh = dxn * gain_ref[...].reshape(1, C)
    m1 = jnp.sum(dxh, axis=1, keepdims=True) * (1.0 / C)
    m2 = jnp.sum(dxh * xhat, axis=1, keepdims=True) * (1.0 / C)
    out = err_s[...] + inv * (dxh - m1 - xhat * m2)
    for w in range(3):
        gi_ref[49 * w : 49 * w + 49, :] = out[64 * w : 64 * w + 49, :]
    gain = jnp.sum(dxn * xhat, axis=0, keepdims=True)
    sq = err_s[...]
    loss = jnp.sum(sq * sq, axis=0, keepdims=True)
    loss = sum(loss[:, 128 * j : 128 * j + 128] for j in range(6))
    loss = jnp.sum(loss, axis=1, keepdims=True) + jnp.zeros((1, 128), F32)
    tail = jnp.concatenate(
        [gain[:, 128 * j : 128 * j + 128] for j in range(6)] + [loss, jnp.zeros((1, 128), F32)], axis=0
    )

    take(3)
    step(1, 3)
    step(0, 4)

    dtab = jnp.zeros((64, ENT), F32)
    for p in range(16):
        ds = jnp.concatenate([dsum_s.at[j][pl.ds(p, 24, stride=16), :] for j in range(2)], axis=1)
        top = ds.astype(BF16)
        rem = (ds - top.astype(F32)).astype(BF16)
        z8 = jnp.zeros((8, 256), F32)
        both = jnp.concatenate([top.astype(F32), z8, rem.astype(F32), z8], axis=0).astype(BF16)
        dtab = dtab + dot(both, onehot_rows(relp, p), 1, 1)
    dtab = dtab[0:24] + dtab[32:56]
    for g in range(8):
        sm_ref[g] = jnp.zeros((8, 384), F32)
        sm_ref[g, 0:3, 0:ENT] = dtab[3 * g : 3 * g + 3]
        sm_ref[g, :, 256:384] = tail
    for j, peer in enumerate(talk):
        push(sm_ref.at[2 * peer[2] + peer[3]], sm0.at[j], send_s.at[j], recv_s.at[j], peer)

    for b in range(8):
        total = rx[3, b].astype(F32)
        for i in range(3):
            if b == 0:
                landed(cxf.at[i], recv_rx.at[i])
            total = total + cxf[i, b].astype(F32)
        rx[3, b] = total.astype(BF16)
    for d in (4, 3, 5, 2, 6, 1, 7):
        push(rx.at[3, shift(z, d, 8)], s2x.at[d - 1], send_2.at[2, d - 1], recv_2.at[2, d - 1], line_z[d - 1])
    step(1, 4)
    finish(0, 0)
    finish(1, 0)
    for j in range(7):
        landed(sm0.at[j], recv_s.at[j])
    ss1[...] = sm_ref[mp] + sum(sm0[j] for j in range(7))
    for j, to in enumerate(line_y):
        push(ss1, sm1.at[j], send_s.at[7 + j], recv_s.at[7 + j], to)
    finish(0, 1)
    finish(1, 1)
    finish(0, 2)
    finish(1, 2)
    finish(0, 3)
    finish(1, 3)
    for j in range(7):
        landed(sm1.at[j], recv_s.at[7 + j])
    ss2[...] = ss1[...] + sum(sm1[j] for j in range(7))
    for j, to in enumerate(line_z):
        push(ss2, sm2.at[j], send_s.at[14 + j], recv_s.at[14 + j], to)

    a3[...] = jnp.zeros_like(a3)
    b3[...] = jnp.zeros_like(b3)

    def collect(num, r, me, buf):
        total = r[3, me].astype(F32)
        for i in range(3):
            landed(buf.at[i], recv_2.at[num, i])
            total = total + buf[i].astype(F32)
        flat[num] = total

    def spread_out(src, me, dst, num, reach):
        for d in (4, 3, 5, 2, 6, 1, 7, 0):
            for k, core in enumerate((c, 1 - c)):
                if d or k:
                    push(src.at[shift(me, d, 8)], dst.at[k, d], send_3.at[num, k, d], recv_3.at[num, k, d],
                         reach(d, core))

    def gathered(src, me, dst, num, k):
        total = src[me] if k == 0 else 0.0
        for d in (0, 1, 7, 2, 6, 3, 5, 4):
            if d or k:
                landed(dst.at[k, d], recv_3.at[num, k, d])
                total = total + dst[k, d]
        return total

    collect(0, ry, y, s2y)
    for i in range(8):
        a3[i, 0:12, :] = flat[0, 12 * i : 12 * i + 12, :]
    spread_out(a3, z, r3a, 0, lambda d, core: (shift(z, d, 8), y, x, core))
    collect(1, rz, z, s2z)
    for i in range(8):
        b3[i, 1, 0:12, :] = flat[1, 12 * i : 12 * i + 12, :]
    total = rx[3, z].astype(F32)
    for j in range(7):
        landed(s2x.at[j], recv_2.at[2, j])
        total = total + s2x[j].astype(F32)
    flat[2] = total
    for i in range(8):
        b3[i, 0, 0:12, :] = flat[2, 12 * i : 12 * i + 12, :]
    spread_out(b3, y, r3b, 1, lambda d, core: (z, shift(y, d, 8), x, core))

    total = ss2[...]
    for j in range(7):
        landed(sm2.at[j], recv_s.at[14 + j])
        total = total + sm2[j]
    gtab_ref[...] = total[0:3, 0:TABLE] * shrink
    for j in range(6):
        ggain_ref[pl.ds(128 * j, 128)] = total[j : j + 1, 256:384].reshape(128) * shrink
    loss_ref[...] = total[6:7, 256:384] * (0.5 / count)
    for k, core in enumerate((c, 1 - c)):
        part_s[core, :, 0:128] = gathered(a3, z, r3a, 0, k)
    for k, core in enumerate((c, 1 - c)):
        total = gathered(b3, y, r3b, 1, k)
        part_s[core, :, 128:256] = total[0]
        part_s[core, :, 256:384] = total[1]
    for t in range(4):
        at = 192 * (t % 2)
        both = part_s[t // 2, 0:12, :] * shrink
        mine = jnp.where(c == 0, both[:, at : at + 96], both[:, at + 96 : at + 192])
        if t < 3:
            gq_ref[t] = mine
        else:
            gp_ref[...] = mine
    for copy in started:
        copy.wait_send()


def whole(count, *args):
    dma = pltpu.SemaphoreType.DMA
    f = lambda *s: pltpu.VMEM(s, F32)
    b = lambda *s: pltpu.VMEM(s, BF16)
    shape = jax.ShapeDtypeStruct
    return pl.pallas_call(
        functools.partial(whole_kernel, count),
        name="window_layer",
        out_shape=(
            shape((147, C), F32), shape((3, 12, 96), F32), shape((12, 96), F32),
            shape((3, TABLE), F32), shape((C,), F32), shape((1, 128), F32),
        ),
        in_specs=[pl.BlockSpec(memory_space=pltpu.HBM)] * 8,
        out_specs=(VM,) * 6,
        scratch_shapes=[
            b(147, C), b(147, C), pltpu.VMEM((24, 49), jnp.int32), pltpu.VMEM((49, 49), jnp.int32), f(C), f(3, TABLE),
            f(8, 256), b(4, 4, 2, 96, C), f(8, 8, 256),
            dma((2, 2)), dma((2, 2)), dma((2,)), dma((2,)), dma((3, 2, 4)), dma((3, 2, 4)),
            dma((34,)), dma((34,)), dma((7,)), dma((7,)), dma((10,)),
            f(152, C), f(192, C), f(192, C), f(192, C), b(192, C), b(C, 384), f(C, 192), b(C, 192),
            f(192, C), f(192, C), b(192, C), f(192, C),
            pltpu.VMEM((64, 128), jnp.int32), f(2, 384, 128), f(4, 64, 384), f(4, 3, 64, 384),
            b(4, 192, 192), b(4, 192, 192), b(4, 192, 192), b(4, 192, 192), f(2, 384, 128), f(8, 8, 384),
            b(2, 4, 8, 96, 128), b(2, 4, 8, 96, 128), b(2, 4, 8, 96, 128),
            b(4, 8, 96, 128), b(4, 8, 96, 128), b(4, 8, 96, 128),
            b(2, 4, 2, 96, 128), b(2, 4, 2, 96, 128), b(2, 7, 96, 128), b(2, 7, 96, 128), b(3, 8, 96, 128),
            b(3, 96, 128), b(3, 96, 128), b(7, 96, 128), f(3, 96, 128),
            f(8, 16, 128), f(8, 2, 16, 128), f(2, 8, 16, 128), f(2, 8, 2, 16, 128), f(2, 16, 384),
            f(7, 8, 384), f(7, 8, 384), f(7, 8, 384), f(8, 384), f(8, 384),
            dma((3, 4)), dma((3, 4)), dma((2, 2, 4, 2)), dma((2, 2, 4, 2)), dma((2, 2, 7)), dma((2, 2, 7)), dma((3,)), dma((3,)),
            dma((3, 7)), dma((3, 7)), dma((2, 2, 8)), dma((2, 2, 8)), dma((21,)), dma((21,)),
        ],
        compiler_params=pltpu.CompilerParams(
            collective_id=0, has_side_effects=True, vmem_limit_bytes=40 * 2**20
        ),
    )(*args)


def hand_out_kernel(*refs):
    copies = [pltpu.make_async_copy(refs[k], refs[6 + k], refs[12].at[k]) for k in range(6)]
    for copy in copies:
        copy.start()
    for copy in copies:
        copy.wait()


def hand_out(*arrays):
    return pl.pallas_call(
        hand_out_kernel,
        name="hand_out",
        out_shape=tuple(jax.ShapeDtypeStruct(a.shape, a.dtype) for a in arrays),
        in_specs=[VM] * 6,
        out_specs=(pl.BlockSpec(memory_space=pl.ANY),) * 6,
        scratch_shapes=[pltpu.SemaphoreType.DMA((6,))],
        compiler_params=pltpu.CompilerParams(vmem_limit_bytes=8 * 2**20),
    )(*arrays)


def per_device(tokens, target, regions, rel_index, layer_norm_gain, bias_table, w_qkv, w_proj):
    count = tokens.shape[0] * lax.axis_size(DP_WIN_MP)
    args = (tokens, target, regions, rel_index, layer_norm_gain, bias_table.T, w_qkv, w_proj)
    done = whole(count, *[pltpu.with_memory_space_constraint(one, pltpu.HBM) for one in args])
    gi, gq, gp, gtab, ggain, loss = hand_out(*done)
    return gi, jnp.transpose(gq, (0, 2, 1)), gp.T, gtab.T, ggain, loss[0, 0]


def solution(mesh):
    split = Mesh(mesh.devices.reshape(mesh.shape["dp"], mesh.shape["win"], 4, 2), DP_WIN_MP)
    return jax.shard_map(
        per_device,
        mesh=split,
        in_specs=(
            P(DP_WIN_MP, None), P(DP_WIN_MP, None), P(("dp", "win"), None), P(), P(),
            P(None, MP), P(None, MP, None), P(MP, None),
        ),
        out_specs=(
            P(DP_WIN_MP, None), P(None, MP, ("dp", "win")), P(MP, ("dp", "win")), P(None, MP), P(), P(),
        ),
        check_vma=False,
    )
```

time: 262 us -> 79.1 us (0.30)
  blocking collectives: 97.4 us -> 0 us
  Pallas kernels: 0 us -> 78.2 us
  waiting for transfers between devices: 56 us -> 0 us
  starting transfers between devices: 41.2 us -> 0 us
  local copies, waits for them, and re-layouts: 27.7 us -> 0 us
  matrix products: 20.4 us -> 0 us
  other arithmetic: 13.9 us -> 0 us
  between operations: 3.64 us -> 0.8 us
    pallas_call x0 -> x2, Pallas kernels: none -> 78.2 us  [the longest x1 77.4 us: whole(): pl.pallas_call(functools.partial(whole_kernel, count), name='window_layer...]
    all_to_all x6 -> x0, waiting for transfers between devices: 56 us -> none  [the longest x2 42.2 us: from_everyone(): lax.all_to_all(jnp.broadcast_to(value[None], (count, *value.shape)), axis...]
    psum x4 -> x0, blocking collectives: 52.6 us -> none  [by_axis(): return functools.reduce(lax.psum, axes, value)]
    all_to_all x6 -> x0, starting transfers between devices: 37.9 us -> none  [the longest x4 22.6 us: sent_and_summed(): blocks = lax.all_to_all(split_up(value, dim, count), axis, 0, 0, tiled=True)]
    all_to_all x1 -> x0, blocking collectives: 27.5 us -> none  [sent_and_summed(): blocks = lax.all_to_all(split_up(value, dim, count), axis, 0, 0, tiled=True)]
    dot_general x13 -> x0, matrix products: 17.9 us -> none  [the longest x1 2.81 us: per_device(): jnp.einsum('trh,rc->thc', dqkv, normed_input, preferred_element_type=f32)]
    unnamed x1 -> x0, blocking collectives: 17.3 us -> none
    reshape x11 -> x0, local copies, waits for them, and re-layouts: 8.98 us -> none  [the longest x7 5.21 us: split_up(): return jnp.moveaxis(value.reshape(*before, count, -1, *after), dim, 0)]
  transfers between devices with their start and end apart: 7 -> 0, of which waited for: 4 -> 0; matrix products, arithmetic and copies ran while one was open for 13% -> 0% of each run, Pallas kernels for 0% -> 0%
where the time goes in v3:
time: 79.1 us; the launch traced here: 79 us
  Pallas kernels  78.2 us (99%)
  between operations  0.8 us (1%)
    pallas_call x1, Pallas kernels, whole(): pl.pallas_call(functools.partial(whole_kernel, count), name='window_layer...  77.4 us

profile of v3, /device:TPU:1, one launch (start us, length us, event | category | flops | bytes accessed | tf_op | source)
XLA Modules:
  0.0 79.0 jit_solution(180994539563815469)
XLA Ops:
  0.6 77.4 %window_layer.1 = (f32[147,768]{1,0:T(8,128)S(1)}, f32[3,12,96]{2,1,0:T(8,128)S(1)}, f32[12,96]{1,0:T(8,128)S(1)}, f32[3,169]{1,0:T(4,128)S(1)}, f32[768]{0:T(1024)S(1)}, /*index=5*/f32[1,128]{1,0:T(1,128)S(1)}) custom-call(bf16[147,768]{1,0:T(8,128)(2,1)} %refs_0_.1, bf16[147,768]{1,0:T(8,128)(2,1)} %refs_1_.1, s32[24,49]{1,0:T(8,128)} %refs_2_.1, ...), custom_call_target="tpu_custom_call" | custom-call | tf_op jit(solution)/shard_map/window_layer/pallas_call | solution.py:565
  78.0 0.8 %hand_out.1 = (f32[147,768]{1,0:T(8,128)}, f32[3,12,96]{2,1,0:T(8,128)}, f32[12,96]{1,0:T(8,128)}, f32[3,169]{1,0:T(4,128)}, f32[768]{0:T(1024)}, /*index=5*/f32[1,128]{1,0:T(1,128)}) custom-call(f32[147,768]{1,0:T(8,128)S(1)} %get-tuple-element.18.refs_0_, f32[3,12,96]{2,1,0:T(8,128)S(1)} %get-tuple-element.19.refs_1_, ...), custom_call_target="tpu_custom_call" | custom-call | tf_op jit(solution)/shard_map/hand_out/pallas_call | solution.py:607

commit v4 on v3

--- a/solution.py
+++ b/solution.py
@@ -41,12 +41,11 @@
         tok_hbm, tgt_hbm, reg_hbm, rel_hbm, gain_hbm, table_hbm, wqkv_hbm, wproj_hbm,
         gi_ref, gq_ref, gp_ref, gtab_ref, ggain_ref, loss_ref,
         tok_ref, tgt_ref, reg_ref, rel_ref, gain_ref, table_ref, tab_s, w_ref, t_ref,
-        send_x, recv_x, send_o, recv_o, send_n, recv_n, send_c, recv_c, send_t, recv_t, own_sem,
+        send_w, recv_x, recv_o, recv_n, send_c, recv_c, send_t, recv_t, own_sem,
         pad_s, x_s, t_s, xh_s, xn_s, xt_s, xtf_s, xtp_s, ysum_s, err_s, gb_s, dxn_s,
         relp_s, bt_s, bias_s, p_s, q_s, k_s, v_s, at_s, dsum_s, sm_ref,
-        gy_s, gz_s, gx_s, ry, rz, rx, cy, cz, dy, dz, cxf,
-        s2y, s2z, s2x, flat, a3, b3, r3a, r3b, part_s, sm0, sm1, sm2, ss1, ss2,
-        send_d, recv_d, send_r, recv_r, send_v, recv_v, send_rx, recv_rx,
+        grads, sums, ring, direct, cxf, s2, s2x, flat, a3, b3, r3a, r3b, part_s, sm0, sm1, sm2, ss1, ss2,
+        send_d, recv_d, send_v, recv_r, recv_v, send_rx, recv_rx,
         send_2, recv_2, send_3, recv_3, send_s, recv_s,
     ) = refs
     z, y, x, c = (lax.axis_index(name) for name in DP_WIN_MP)
@@ -58,19 +57,20 @@
     line_y = [(z, shift(y, d, 8), x, c) for d in range(1, 8)]
     line_z = [(shift(z, d, 8), y, x, c) for d in range(1, 8)]
     line_x = [(z, y, shift(x, d, 4), c) for d in range(1, 4)]
-    started = []
-
     def push(src, dst, ssem, rsem, to):
-        copy = pltpu.make_async_remote_copy(
+        pltpu.make_async_remote_copy(
             src_ref=src, dst_ref=dst, send_sem=ssem, recv_sem=rsem, device_id=to, device_id_type=MESH
-        )
-        copy.start()
-        started.append(copy)
+        ).start()
 
     def landed(dst, rsem):
         pltpu.make_async_remote_copy(
             src_ref=dst, dst_ref=dst, send_sem=rsem, recv_sem=rsem, device_id=partner, device_id_type=MESH
         ).wait_recv()
+
+    def left_here(amount, ssem):
+        pltpu.make_async_remote_copy(
+            src_ref=amount, dst_ref=amount, send_sem=ssem, recv_sem=ssem, device_id=partner, device_id_type=MESH
+        ).wait_send()
 
     barrier = pltpu.get_barrier_semaphore()
     peers = talk + line_y + line_z
@@ -135,13 +135,13 @@
     for m in range(2):
         for j, d in enumerate((1, -1)):
             there = piece(x, colors[m], c, m)
-            push(there, there, send_x.at[m, j], recv_x.at[m, j], (z, y, shift(x, d, 4), c))
+            push(there, there, send_w.at[0], recv_x.at[m], (z, y, shift(x, d, 4), c))
         if m == 0:
-            for j, to in enumerate(talk):
-                push(tab_s, t_ref.at[mp], send_t.at[j], recv_t.at[j], to)
+            for to in talk:
+                push(tab_s, t_ref.at[mp], send_t.at[0], recv_t.at[0], to)
     for one in range(4):
         there = w_ref.at[x, one, c]
-        push(there, there, send_c.at[one], recv_c.at[one], partner)
+        push(there, there, send_c.at[0], recv_c.at[3], partner)
     load[8].wait()
     load[9].wait()
 
@@ -178,26 +178,21 @@
         xs = sources[slot]
         tint = colors[m]
         for j in range(2):
-            push(piece(xs, tint, c, m), piece(xs, tint, c, m),
-                 send_n.at[slot, m, j], recv_n.at[slot, m, j], strong[m][j])
+            push(piece(xs, tint, c, m), piece(xs, tint, c, m), send_w.at[0], recv_n.at[slot], strong[m][j])
         for j in range(2):
-            push(lanes(xs, tint, c, m, j), lanes(xs, tint, c, m, j),
-                 send_n.at[slot, m, 2 + j], recv_n.at[slot, m, 2 + j], weak[m][j])
-        push(piece(xs, tint, c, m), piece(xs, tint, c, m),
-             send_c.at[4 + 10 * slot + 5 * m], recv_c.at[4 + 10 * slot + 5 * m], partner)
-
-    for m in range(2):
+            push(lanes(xs, tint, c, m, j), lanes(xs, tint, c, m, j), send_w.at[0], recv_n.at[slot], weak[m][j])
+        push(piece(xs, tint, c, m), piece(xs, tint, c, m), send_c.at[0], recv_c.at[slot], partner)
+
+    def from_sides(m):
+        landed(w_ref.at[left, 0, c], recv_x.at[m])
+        there = piece(sources[m], colors[m], c, m)
+        push(there, there, send_w.at[0], recv_o.at[m], (z, y, shift(x, 1 - 2 * m, 4), c))
         for slot in range(2):
-            landed(piece(sources[slot], colors[m], c, m), recv_x.at[m, slot])
-            if slot == m:
-                there = piece(sources[slot], colors[m], c, m)
-                push(there, there, send_o.at[m], recv_o.at[m], (z, y, shift(x, 1 - 2 * slot, 4), c))
             hand_on(slot, m)
 
-    landed(t_ref.at[2 * x + 1 - c], recv_t.at[0])
-    for d in (1, 2, 3):
-        landed(t_ref.at[2 * shift(x, -d, 4) + c], recv_t.at[2 * d - 1])
-        landed(t_ref.at[2 * shift(x, -d, 4) + 1 - c], recv_t.at[2 * d])
+    from_sides(0)
+
+    landed(t_ref.at[pl.ds(0, 7)], recv_t.at[0])
     tab = jnp.concatenate([t_ref[g, 0:3, 0:ENT] for g in range(8)], axis=0)
     hi = tab.astype(BF16)
     rest = tab - hi.astype(F32)
@@ -259,35 +254,25 @@
 
     def hand_over(slot):
         xs = sources[slot]
+        landed(w_ref.at[xs, pl.ds(0, 3), c], recv_n.at[slot])
         for m in range(2):
             tints, across = near_tints(m)
             for j in range(2):
                 there = piece(xs, tints[j], c, m)
-                landed(there, recv_n.at[slot, m, j])
-                at = 5 + 10 * slot + 5 * m + j
-                push(there, there, send_c.at[at], recv_c.at[at], partner)
+                push(there, there, send_c.at[0], recv_c.at[slot], partner)
             for j in range(2):
                 there = lanes(xs, across, c, m, j)
-                landed(there, recv_n.at[slot, m, 2 + j])
-                at = 7 + 10 * slot + 5 * m + j
-                push(there, there, send_c.at[at], recv_c.at[at], partner)
+                push(there, there, send_c.at[0], recv_c.at[slot], partner)
 
     def whole_slot(slot):
-        xs = sources[slot]
-        for m in range(2):
-            tints, across = near_tints(m)
-            at = 4 + 10 * slot + 5 * m
-            landed(piece(xs, colors[m], 1 - c, m), recv_c.at[at])
-            for j in range(2):
-                landed(piece(xs, tints[j], 1 - c, m), recv_c.at[at + 1 + j])
-                landed(lanes(xs, across, 1 - c, m, j), recv_c.at[at + 3 + j])
-
+        landed(w_ref.at[sources[slot], :, 1 - c], recv_c.at[slot])
+
+    landed(w_ref.at[x, :, 1 - c], recv_c.at[3])
+    forward(3, x, True)
+    from_sides(1)
     for m in range(2):
         landed(piece(opposite, colors[m], c, m), recv_o.at[m])
         hand_on(2, m)
-    for one in range(4):
-        landed(w_ref.at[x, one, 1 - c], recv_c.at[one])
-    forward(3, x, True)
     hand_over(0)
     hand_over(1)
     whole_slot(0)
@@ -341,88 +326,80 @@
         for b in range(8):
             rows = slice(96 * b, 96 * b + 96)
             one = dot(xtp_s[rows, :], lead, 1, 0).astype(BF16)
-            gy_s[0, i, b] = one[:, 0:128]
-            gy_s[1, i, b] = one[:, 128:256]
+            grads[0, 0, i, b] = one[:, 0:128]
+            grads[0, 1, i, b] = one[:, 128:256]
             two = dot(xt_s[rows, 0:192], low_half, 1, 0).astype(BF16)
-            gx_s[0, i, b] = two[:, 0:128]
-            gz_s[0, i, b] = two[:, 128:256]
+            grads[2, 0, i, b] = two[:, 0:128]
+            grads[1, 0, i, b] = two[:, 128:256]
             three = dot(xt_s[rows, :], high_half, 1, 0).astype(BF16)
-            gx_s[1, i, b] = three[:, 0:128]
-            gz_s[1, i, b] = three[:, 128:256]
-        for num, (g, r) in enumerate(((gy_s, ry), (gz_s, rz), (gx_s, rx))):
-            push(g.at[1 - c, i], r.at[i], send_d.at[num, i], recv_d.at[num, i], partner)
+            grads[2, 1, i, b] = three[:, 0:128]
+            grads[1, 1, i, b] = three[:, 128:256]
+        for num in range(3):
+            push(grads.at[num, 1 - c, i], sums.at[num, i], send_d.at[0], recv_d.at[i], partner)
         part = (
             dot(dqb, weight(xs, 0), 1, 0) + dot(dkb, weight(xs, 1), 1, 0) + dot(dvb, weight(xs, 2), 1, 0)
         )
         dxn_s[...] = part if first else dxn_s[...] + part
 
-    direct = (dy, dz)
-    rings = (
-        (0, gy_s, ry, cy, y, lambda d: (z, shift(y, d, 8), x, c)),
-        (1, gz_s, rz, cz, z, lambda d: (shift(z, d, 8), y, x, c)),
+    lines = (
+        (0, y, lambda d: (z, shift(y, d, 8), x, c)),
+        (1, z, lambda d: (shift(z, d, 8), y, x, c)),
     )
+    far_first = (4, 3, 5, 2, 6, 1, 7)
 
     def take(i):
-        for num, g, r, ring, me, reach in rings:
-            landed(r.at[i], recv_d.at[num, i])
+        landed(sums.at[:, i], recv_d.at[i])
+        for num in range(3):
             for b in range(8):
-                r[i, b] = r[i, b] + g[c, i, b]
-            if i < 2:
+                sums[num, i, b] = sums[num, i, b] + grads[num, c, i, b]
+        if i < 3:
+            push(sums.at[2, i], cxf.at[i], send_rx.at[0], recv_rx.at[0], (z, y, order[i], c))
+        if i == 0:
+            for num, me, reach in lines:
                 far = shift(me, 4, 8)
                 for way, sign in enumerate((1, -1)):
-                    push(r.at[i, far, rows_of(way)], ring.at[way, 0, i, rows_of(way)],
-                         send_r.at[num, way, 0, i], recv_r.at[num, way, 0, i], reach(sign))
-            else:
-                for d in (4, 3, 5, 2, 6, 1, 7):
-                    push(r.at[i, shift(me, d, 8)], direct[num].at[i - 2, d - 1],
-                         send_v.at[num, i - 2, d - 1], recv_v.at[num, i - 2, d - 1], reach(d))
-        landed(rx.at[i], recv_d.at[2, i])
-        for b in range(8):
-            rx[i, b] = rx[i, b] + gx_s[c, i, b]
-        if i < 3:
-            push(rx.at[i], cxf.at[i], send_rx.at[i], recv_rx.at[i], (z, y, order[i], c))
-
-    def step(i, s):
-        for num, g, r, ring, me, reach in rings:
+                    push(sums.at[num, 0, far, rows_of(way)], ring.at[num, way, 0, rows_of(way)],
+                         send_v.at[0], recv_r.at[0], reach(sign))
+        else:
+            for d in far_first:
+                for num, me, reach in lines:
+                    push(sums.at[num, i, shift(me, d, 8)], direct.at[num, i - 1, d - 1],
+                         send_v.at[0], recv_v.at[i - 1], reach(d))
+
+    def step(s):
+        landed(ring.at[0, :, 0] if s == 2 else ring.at[:, :, s - 2], recv_r.at[s - 2])
+        for num, me, reach in lines:
             for way, sign in enumerate((1, -1)):
                 block = shift(me, sign * (5 - s), 8)
-                if s == 2:
-                    landed(ring.at[way, 0, i, rows_of(way)], recv_r.at[num, way, 0, i])
-                    cut = slice(48 * way, 48 * way + 48)
-                    r[i, block, cut, :] = r[i, block, cut, :] + ring[way, 0, i, cut, :]
-                else:
-                    landed(ring.at[way, s - 2, i], recv_r.at[num, way, s - 2, i])
-                    r[i, block] = r[i, block] + ring[way, s - 2, i]
-                push(r.at[i, block], ring.at[way, s - 1, i],
-                     send_r.at[num, way, s - 1, i], recv_r.at[num, way, s - 1, i], reach(sign))
-
-    def finish(num, i):
-        num, g, r, ring, me, reach = rings[num]
-        if i < 2:
-            for way in range(2):
-                landed(ring.at[way, 3, i], recv_r.at[num, way, 3, i])
-            total = r[i, me].astype(F32) + ring[0, 3, i].astype(F32) + ring[1, 3, i].astype(F32)
+                rows = slice(48 * way, 48 * way + 48) if s == 2 else slice(0, 96)
+                sums[num, 0, block, rows, :] = sums[num, 0, block, rows, :] + ring[num, way, s - 2, rows, :]
+                push(sums.at[num, 0, block], ring.at[num, way, s - 1], send_v.at[0], recv_r.at[s - 1], reach(sign))
+
+    def finish(i):
+        if i == 0:
+            landed(ring.at[:, :, 3], recv_r.at[3])
         else:
-            total = r[i, me].astype(F32)
-            for d in (1, 7, 2, 6, 3, 5, 4):
-                landed(direct[num].at[i - 2, d - 1], recv_v.at[num, i - 2, d - 1])
-                total = total + direct[num][i - 2, d - 1].astype(F32)
-        r[i, me] = total.astype(BF16)
-        buf = (s2y, s2z)[num]
-        if i < 3:
-            to = (z, y, order[i], c)
-            push(r.at[i, me], buf.at[i], send_2.at[num, i], recv_2.at[num, i], to)
+            landed(direct.at[:, i - 1], recv_v.at[i - 1])
+        for num, me, reach in lines:
+            total = sums[num, i, me].astype(F32)
+            if i == 0:
+                total = total + ring[num, 0, 3].astype(F32) + ring[num, 1, 3].astype(F32)
+            else:
+                for d in range(1, 8):
+                    total = total + direct[num, i - 1, d - 1].astype(F32)
+            sums[num, i, me] = total.astype(BF16)
+            if i < 3:
+                push(sums.at[num, i, me], s2.at[num, i], send_2.at[0], recv_2.at[0], (z, y, order[i], c))
 
     backward(0, True)
     backward(1, False)
     take(0)
     backward(2, False)
+    step(2)
     take(1)
-    step(0, 2)
     backward(3, False)
+    step(3)
     take(2)
-    step(1, 2)
-    step(0, 3)
 
     dxn = dxn_s[...]
     xhat = xh_s[...]
@@ -441,10 +418,6 @@
         [gain[:, 128 * j : 128 * j + 128] for j in range(6)] + [loss, jnp.zeros((1, 128), F32)], axis=0
     )
 
-    take(3)
-    step(1, 3)
-    step(0, 4)
-
     dtab = jnp.zeros((64, ENT), F32)
     for p in range(16):
         ds = jnp.concatenate([dsum_s.at[j][pl.ds(p, 24, stride=16), :] for j in range(2)], axis=1)
@@ -459,90 +432,79 @@
         sm_ref[g, 0:3, 0:ENT] = dtab[3 * g : 3 * g + 3]
         sm_ref[g, :, 256:384] = tail
     for j, peer in enumerate(talk):
-        push(sm_ref.at[2 * peer[2] + peer[3]], sm0.at[j], send_s.at[j], recv_s.at[j], peer)
-
+        push(sm_ref.at[2 * peer[2] + peer[3]], sm0.at[j], send_s.at[0], recv_s.at[0], peer)
+
+    step(4)
+    take(3)
+    landed(cxf, recv_rx.at[0])
     for b in range(8):
-        total = rx[3, b].astype(F32)
+        total = sums[2, 3, b].astype(F32)
         for i in range(3):
-            if b == 0:
-                landed(cxf.at[i], recv_rx.at[i])
             total = total + cxf[i, b].astype(F32)
-        rx[3, b] = total.astype(BF16)
-    for d in (4, 3, 5, 2, 6, 1, 7):
-        push(rx.at[3, shift(z, d, 8)], s2x.at[d - 1], send_2.at[2, d - 1], recv_2.at[2, d - 1], line_z[d - 1])
-    step(1, 4)
-    finish(0, 0)
-    finish(1, 0)
-    for j in range(7):
-        landed(sm0.at[j], recv_s.at[j])
+        sums[2, 3, b] = total.astype(BF16)
+    for d in far_first:
+        push(sums.at[2, 3, shift(z, d, 8)], s2x.at[d - 1], send_2.at[1], recv_2.at[1], line_z[d - 1])
+    landed(sm0, recv_s.at[0])
     ss1[...] = sm_ref[mp] + sum(sm0[j] for j in range(7))
     for j, to in enumerate(line_y):
-        push(ss1, sm1.at[j], send_s.at[7 + j], recv_s.at[7 + j], to)
-    finish(0, 1)
-    finish(1, 1)
-    finish(0, 2)
-    finish(1, 2)
-    finish(0, 3)
-    finish(1, 3)
-    for j in range(7):
-        landed(sm1.at[j], recv_s.at[7 + j])
+        push(ss1, sm1.at[j], send_s.at[1], recv_s.at[1], to)
+    for i in range(4):
+        finish(i)
+    landed(sm1, recv_s.at[1])
     ss2[...] = ss1[...] + sum(sm1[j] for j in range(7))
     for j, to in enumerate(line_z):
-        push(ss2, sm2.at[j], send_s.at[14 + j], recv_s.at[14 + j], to)
+        push(ss2, sm2.at[j], send_s.at[2], recv_s.at[2], to)
 
     a3[...] = jnp.zeros_like(a3)
     b3[...] = jnp.zeros_like(b3)
 
-    def collect(num, r, me, buf):
-        total = r[3, me].astype(F32)
+    def collect(num, me):
+        total = sums[num, 3, me].astype(F32)
         for i in range(3):
-            landed(buf.at[i], recv_2.at[num, i])
-            total = total + buf[i].astype(F32)
+            total = total + s2[num, i].astype(F32)
         flat[num] = total
 
     def spread_out(src, me, dst, num, reach):
         for d in (4, 3, 5, 2, 6, 1, 7, 0):
             for k, core in enumerate((c, 1 - c)):
                 if d or k:
-                    push(src.at[shift(me, d, 8)], dst.at[k, d], send_3.at[num, k, d], recv_3.at[num, k, d],
-                         reach(d, core))
-
-    def gathered(src, me, dst, num, k):
-        total = src[me] if k == 0 else 0.0
-        for d in (0, 1, 7, 2, 6, 3, 5, 4):
-            if d or k:
-                landed(dst.at[k, d], recv_3.at[num, k, d])
-                total = total + dst[k, d]
+                    push(src.at[shift(me, d, 8)], dst.at[8 * k + d - 1], send_3.at[num], recv_3.at[num], reach(d, core))
+
+    def gathered(src, me, dst, k):
+        total = src[me] if k == 0 else dst[7]
+        for d in range(1, 8):
+            total = total + dst[8 * k + d - 1]
         return total
 
-    collect(0, ry, y, s2y)
+    landed(s2, recv_2.at[0])
+    collect(0, y)
     for i in range(8):
         a3[i, 0:12, :] = flat[0, 12 * i : 12 * i + 12, :]
     spread_out(a3, z, r3a, 0, lambda d, core: (shift(z, d, 8), y, x, core))
-    collect(1, rz, z, s2z)
+    collect(1, z)
     for i in range(8):
         b3[i, 1, 0:12, :] = flat[1, 12 * i : 12 * i + 12, :]
-    total = rx[3, z].astype(F32)
+    landed(s2x, recv_2.at[1])
+    total = sums[2, 3, z].astype(F32)
     for j in range(7):
-        landed(s2x.at[j], recv_2.at[2, j])
         total = total + s2x[j].astype(F32)
     flat[2] = total
     for i in range(8):
         b3[i, 0, 0:12, :] = flat[2, 12 * i : 12 * i + 12, :]
     spread_out(b3, y, r3b, 1, lambda d, core: (z, shift(y, d, 8), x, core))
 
-    total = ss2[...]
-    for j in range(7):
-        landed(sm2.at[j], recv_s.at[14 + j])
-        total = total + sm2[j]
+    landed(sm2, recv_s.at[2])
+    total = ss2[...] + sum(sm2[j] for j in range(7))
     gtab_ref[...] = total[0:3, 0:TABLE] * shrink
     for j in range(6):
         ggain_ref[pl.ds(128 * j, 128)] = total[j : j + 1, 256:384].reshape(128) * shrink
     loss_ref[...] = total[6:7, 256:384] * (0.5 / count)
+    landed(r3a, recv_3.at[0])
     for k, core in enumerate((c, 1 - c)):
-        part_s[core, :, 0:128] = gathered(a3, z, r3a, 0, k)
+        part_s[core, :, 0:128] = gathered(a3, z, r3a, k)
+    landed(r3b, recv_3.at[1])
     for k, core in enumerate((c, 1 - c)):
-        total = gathered(b3, y, r3b, 1, k)
+        total = gathered(b3, y, r3b, k)
         part_s[core, :, 128:256] = total[0]
         part_s[core, :, 256:384] = total[1]
     for t in range(4):
@@ -553,8 +515,18 @@
             gq_ref[t] = mine
         else:
             gp_ref[...] = mine
-    for copy in started:
-        copy.wait_send()
+    left_here(w_ref.at[:, pl.ds(0, 3), 0], send_w.at[0])
+    left_here(w_ref.at[:, :, 0], send_c.at[0])
+    left_here(t_ref.at[pl.ds(0, 7)], send_t.at[0])
+    left_here(grads.at[:, 0], send_d.at[0])
+    left_here(grads.at[0, :, :, pl.ds(0, 7)], send_v.at[0])
+    left_here(cxf, send_rx.at[0])
+    left_here(s2, send_2.at[0])
+    left_here(s2x, send_2.at[1])
+    left_here(r3a, send_3.at[0])
+    left_here(r3b, send_3.at[1])
+    for k, amount in enumerate((sm0, sm1, sm2)):
+        left_here(amount, send_s.at[k])
 
 
 def whole(count, *args):
@@ -574,20 +546,17 @@
         scratch_shapes=[
             b(147, C), b(147, C), pltpu.VMEM((24, 49), jnp.int32), pltpu.VMEM((49, 49), jnp.int32), f(C), f(3, TABLE),
             f(8, 256), b(4, 4, 2, 96, C), f(8, 8, 256),
-            dma((2, 2)), dma((2, 2)), dma((2,)), dma((2,)), dma((3, 2, 4)), dma((3, 2, 4)),
-            dma((34,)), dma((34,)), dma((7,)), dma((7,)), dma((10,)),
+            dma((1,)), dma((2,)), dma((2,)), dma((3,)), dma((1,)), dma((4,)), dma((1,)), dma((1,)), dma((10,)),
             f(152, C), f(192, C), f(192, C), f(192, C), b(192, C), b(C, 384), f(C, 192), b(C, 192),
             f(192, C), f(192, C), b(192, C), f(192, C),
             pltpu.VMEM((64, 128), jnp.int32), f(2, 384, 128), f(4, 64, 384), f(4, 3, 64, 384),
             b(4, 192, 192), b(4, 192, 192), b(4, 192, 192), b(4, 192, 192), f(2, 384, 128), f(8, 8, 384),
-            b(2, 4, 8, 96, 128), b(2, 4, 8, 96, 128), b(2, 4, 8, 96, 128),
-            b(4, 8, 96, 128), b(4, 8, 96, 128), b(4, 8, 96, 128),
-            b(2, 4, 2, 96, 128), b(2, 4, 2, 96, 128), b(2, 7, 96, 128), b(2, 7, 96, 128), b(3, 8, 96, 128),
-            b(3, 96, 128), b(3, 96, 128), b(7, 96, 128), f(3, 96, 128),
-            f(8, 16, 128), f(8, 2, 16, 128), f(2, 8, 16, 128), f(2, 8, 2, 16, 128), f(2, 16, 384),
+            b(3, 2, 4, 8, 96, 128), b(3, 4, 8, 96, 128), b(2, 2, 4, 96, 128), b(2, 3, 7, 96, 128),
+            b(3, 8, 96, 128), b(2, 3, 96, 128), b(7, 96, 128), f(3, 96, 128),
+            f(8, 16, 128), f(8, 2, 16, 128), f(15, 16, 128), f(15, 2, 16, 128), f(2, 16, 384),
             f(7, 8, 384), f(7, 8, 384), f(7, 8, 384), f(8, 384), f(8, 384),
-            dma((3, 4)), dma((3, 4)), dma((2, 2, 4, 2)), dma((2, 2, 4, 2)), dma((2, 2, 7)), dma((2, 2, 7)), dma((3,)), dma((3,)),
-            dma((3, 7)), dma((3, 7)), dma((2, 2, 8)), dma((2, 2, 8)), dma((21,)), dma((21,)),
+            dma((1,)), dma((4,)), dma((1,)), dma((4,)), dma((3,)), dma((1,)), dma((1,)),
+            dma((2,)), dma((2,)), dma((2,)), dma((2,)), dma((3,)), dma((3,)),
         ],
         compiler_params=pltpu.CompilerParams(
             collective_id=0, has_side_effects=True, vmem_limit_bytes=40 * 2**20

time: 79.1 us -> 73.1 us (0.924)
  Pallas kernels: 78.2 us -> 72.1 us
    pallas_call x1, Pallas kernels: 77.4 us -> 71.3 us  [whole(): pl.pallas_call(functools.partial(whole_kernel, count), name='window_layer...]
where the time goes in v4:
time: 73.1 us; the launch traced here: 72.9 us
  Pallas kernels  72.1 us (99%)
  between operations  0.8 us (1%)
    pallas_call x1, Pallas kernels, whole(): pl.pallas_call(functools.partial(whole_kernel, count), name='window_layer...  71.3 us

profile of v4, /device:TPU:1, one launch (start us, length us, event | category | flops | bytes accessed | tf_op | source)
XLA Modules:
  0.0 72.9 jit_solution(5536606805132831921)
XLA Ops:
  0.6 71.3 %window_layer.1 = (f32[147,768]{1,0:T(8,128)S(1)}, f32[3,12,96]{2,1,0:T(8,128)S(1)}, f32[12,96]{1,0:T(8,128)S(1)}, f32[3,169]{1,0:T(4,128)S(1)}, f32[768]{0:T(1024)S(1)}, /*index=5*/f32[1,128]{1,0:T(1,128)S(1)}) custom-call(bf16[147,768]{1,0:T(8,128)(2,1)} %refs_0_.1, bf16[147,768]{1,0:T(8,128)(2,1)} %refs_1_.1, s32[24,49]{1,0:T(8,128)} %refs_2_.1, ...), custom_call_target="tpu_custom_call" | custom-call | tf_op jit(solution)/shard_map/window_layer/pallas_call | solution.py:537
  71.9 0.8 %hand_out.1 = (f32[147,768]{1,0:T(8,128)}, f32[3,12,96]{2,1,0:T(8,128)}, f32[12,96]{1,0:T(8,128)}, f32[3,169]{1,0:T(4,128)}, f32[768]{0:T(1024)}, /*index=5*/f32[1,128]{1,0:T(1,128)}) custom-call(f32[147,768]{1,0:T(8,128)S(1)} %get-tuple-element.18.refs_0_, f32[3,12,96]{2,1,0:T(8,128)S(1)} %get-tuple-element.19.refs_1_, ...), custom_call_target="tpu_custom_call" | custom-call | tf_op jit(solution)/shard_map/hand_out/pallas_call | solution.py:576

commit v5 on v4

--- a/solution.py
+++ b/solution.py
@@ -44,8 +44,8 @@
         send_w, recv_x, recv_o, recv_n, send_c, recv_c, send_t, recv_t, own_sem,
         pad_s, x_s, t_s, xh_s, xn_s, xt_s, xtf_s, xtp_s, ysum_s, err_s, gb_s, dxn_s,
         relp_s, bt_s, bias_s, p_s, q_s, k_s, v_s, at_s, dsum_s, sm_ref,
-        grads, sums, ring, direct, cxf, s2, s2x, flat, a3, b3, r3a, r3b, part_s, sm0, sm1, sm2, ss1, ss2,
-        send_d, recv_d, send_v, recv_r, recv_v, send_rx, recv_rx,
+        grads, sums, direct, cxf, s2, s2x, flat, a3, b3, x3, r3a, r3b, r3x, part_s, sm0, sm1, sm2, ss1, ss2,
+        send_d, recv_d, send_v, recv_v, send_rx, recv_rx,
         send_2, recv_2, send_3, recv_3, send_s, recv_s,
     ) = refs
     z, y, x, c = (lax.axis_index(name) for name in DP_WIN_MP)
@@ -92,7 +92,8 @@
         one.start()
     tab_s[...] = jnp.zeros_like(tab_s)
     load[5].wait()
-    tab_s[0:3, 0:TABLE] = table_ref[...]
+    for h in range(3):
+        tab_s[:, 256 * h : 256 * h + TABLE] = table_ref[h : h + 1, :]
     t_ref[mp] = tab_s[...]
     load[0].wait()
     load[6].wait()
@@ -130,15 +131,14 @@
     def lanes(xs, tint, core, m, j):
         return w_ref.at[xs, tint, core, rows_of(m), pl.ds(BIG[j], C // 2)]
 
+    for to in talk:
+        push(tab_s, t_ref.at[mp], send_t.at[0], recv_t.at[0], to)
     for k in range(1, 5):
         load[k].wait()
     for m in range(2):
         for j, d in enumerate((1, -1)):
             there = piece(x, colors[m], c, m)
             push(there, there, send_w.at[0], recv_x.at[m], (z, y, shift(x, d, 4), c))
-        if m == 0:
-            for to in talk:
-                push(tab_s, t_ref.at[mp], send_t.at[0], recv_t.at[0], to)
     for one in range(4):
         there = w_ref.at[x, one, c]
         push(there, there, send_c.at[0], recv_c.at[3], partner)
@@ -150,7 +150,7 @@
     xtf_s[...] = xt
     for b in range(8):
         block = jnp.concatenate([xtf_s[96 * k + 12 * b : 96 * k + 12 * b + 12, :] for k in range(8)], axis=0)
-        xtp_s[96 * b : 96 * b + 96, :] = block.astype(BF16)
+        xtp_s[96 * b : 96 * b + 96, 0:192] = block.astype(BF16)
     relp_s[...] = jnp.full(relp_s.shape, -1, jnp.int32)
     relp_s[0:49, 0:49] = rel_ref[...]
     relp = relp_s[...]
@@ -187,13 +187,12 @@
         landed(w_ref.at[left, 0, c], recv_x.at[m])
         there = piece(sources[m], colors[m], c, m)
         push(there, there, send_w.at[0], recv_o.at[m], (z, y, shift(x, 1 - 2 * m, 4), c))
-        for slot in range(2):
-            hand_on(slot, m)
-
-    from_sides(0)
+        hand_on(0, m)
 
     landed(t_ref.at[pl.ds(0, 7)], recv_t.at[0])
-    tab = jnp.concatenate([t_ref[g, 0:3, 0:ENT] for g in range(8)], axis=0)
+    tab = jnp.concatenate(
+        [t_ref[g, 0:1, 256 * h : 256 * h + ENT] for g in range(8) for h in range(3)], axis=0
+    )
     hi = tab.astype(BF16)
     rest = tab - hi.astype(F32)
     mid = rest.astype(BF16)
@@ -267,9 +266,12 @@
     def whole_slot(slot):
         landed(w_ref.at[sources[slot], :, 1 - c], recv_c.at[slot])
 
+    from_sides(0)
+    from_sides(1)
+    hand_on(1, 0)
+    hand_on(1, 1)
     landed(w_ref.at[x, :, 1 - c], recv_c.at[3])
     forward(3, x, True)
-    from_sides(1)
     for m in range(2):
         landed(piece(opposite, colors[m], c, m), recv_o.at[m])
         hand_on(2, m)
@@ -287,9 +289,14 @@
     err = jnp.where(rowid < WIN_TOK, x_s[...] + ysum_s[...] - t_s[...], 0.0)
     err_s[...] = err
     gb_s[...] = err.astype(BF16)
-    xt_s[:, 192:384] = jnp.transpose(err).astype(BF16)
-
-    def backward(i, first):
+    turned = jnp.transpose(err)
+    xt_s[:, 192:384] = turned.astype(BF16)
+    xtf_s[...] = turned
+    for b in range(8):
+        block = jnp.concatenate([xtf_s[96 * k + 12 * b : 96 * k + 12 * b + 12, :] for k in range(8)], axis=0)
+        xtp_s[96 * b : 96 * b + 96, 192:384] = block.astype(BF16)
+
+    def backward(i, first, middle):
         xs = order[i]
         datt = dot(gb_s[...], weight(xs, 3), 1, 1).astype(BF16)
         dqs, dks, dvs = [], [], []
@@ -313,27 +320,29 @@
         dk = jnp.concatenate(dks, axis=0)
         dv = jnp.concatenate(dvs, axis=0)
         dqb, dkb, dvb = dq.astype(BF16), dk.astype(BF16), dv.astype(BF16)
+        middle()
         lead = jnp.concatenate([dqb[:, 0:128], dvb[:, 0:128]], axis=1)
         low_half = jnp.concatenate([dq[:, 128:192], dk], axis=1).astype(BF16)
         zeros = jnp.zeros((192, 64), F32)
-        high_half = jnp.concatenate(
+        att = at_s[i].astype(F32)
+        mixed = jnp.concatenate(
             [
-                jnp.concatenate([dv[:, 128:192], jnp.zeros((192, 192), F32)], axis=1),
-                jnp.concatenate([zeros, at_s[i].astype(F32)], axis=1),
+                jnp.concatenate([dv[:, 128:192], zeros], axis=1),
+                jnp.concatenate([zeros, att[:, 0:64]], axis=1),
             ],
             axis=0,
         ).astype(BF16)
+        last = att[:, 64:192].astype(BF16)
         for b in range(8):
             rows = slice(96 * b, 96 * b + 96)
-            one = dot(xtp_s[rows, :], lead, 1, 0).astype(BF16)
+            one = dot(xtp_s[rows, 0:192], lead, 1, 0).astype(BF16)
             grads[0, 0, i, b] = one[:, 0:128]
             grads[0, 1, i, b] = one[:, 128:256]
             two = dot(xt_s[rows, 0:192], low_half, 1, 0).astype(BF16)
             grads[2, 0, i, b] = two[:, 0:128]
             grads[1, 0, i, b] = two[:, 128:256]
-            three = dot(xt_s[rows, :], high_half, 1, 0).astype(BF16)
-            grads[2, 1, i, b] = three[:, 0:128]
-            grads[1, 1, i, b] = three[:, 128:256]
+            grads[2, 1, i, b] = dot(xtp_s[rows, :], mixed, 1, 0).astype(BF16)
+            grads[1, 1, i, b] = dot(xt_s[rows, 192:384], last, 1, 0).astype(BF16)
         for num in range(3):
             push(grads.at[num, 1 - c, i], sums.at[num, i], send_d.at[0], recv_d.at[i], partner)
         part = (
@@ -354,52 +363,24 @@
                 sums[num, i, b] = sums[num, i, b] + grads[num, c, i, b]
         if i < 3:
             push(sums.at[2, i], cxf.at[i], send_rx.at[0], recv_rx.at[0], (z, y, order[i], c))
-        if i == 0:
+        for d in far_first:
             for num, me, reach in lines:
-                far = shift(me, 4, 8)
-                for way, sign in enumerate((1, -1)):
-                    push(sums.at[num, 0, far, rows_of(way)], ring.at[num, way, 0, rows_of(way)],
-                         send_v.at[0], recv_r.at[0], reach(sign))
-        else:
-            for d in far_first:
-                for num, me, reach in lines:
-                    push(sums.at[num, i, shift(me, d, 8)], direct.at[num, i - 1, d - 1],
-                         send_v.at[0], recv_v.at[i - 1], reach(d))
-
-    def step(s):
-        landed(ring.at[0, :, 0] if s == 2 else ring.at[:, :, s - 2], recv_r.at[s - 2])
-        for num, me, reach in lines:
-            for way, sign in enumerate((1, -1)):
-                block = shift(me, sign * (5 - s), 8)
-                rows = slice(48 * way, 48 * way + 48) if s == 2 else slice(0, 96)
-                sums[num, 0, block, rows, :] = sums[num, 0, block, rows, :] + ring[num, way, s - 2, rows, :]
-                push(sums.at[num, 0, block], ring.at[num, way, s - 1], send_v.at[0], recv_r.at[s - 1], reach(sign))
+                push(sums.at[num, i, shift(me, d, 8)], direct.at[num, i, d - 1], send_v.at[0], recv_v.at[i], reach(d))
 
     def finish(i):
-        if i == 0:
-            landed(ring.at[:, :, 3], recv_r.at[3])
-        else:
-            landed(direct.at[:, i - 1], recv_v.at[i - 1])
+        landed(direct.at[:, i], recv_v.at[i])
         for num, me, reach in lines:
             total = sums[num, i, me].astype(F32)
-            if i == 0:
-                total = total + ring[num, 0, 3].astype(F32) + ring[num, 1, 3].astype(F32)
-            else:
-                for d in range(1, 8):
-                    total = total + direct[num, i - 1, d - 1].astype(F32)
+            for d in range(1, 8):
+                total = total + direct[num, i, d - 1].astype(F32)
             sums[num, i, me] = total.astype(BF16)
             if i < 3:
                 push(sums.at[num, i, me], s2.at[num, i], send_2.at[0], recv_2.at[0], (z, y, order[i], c))
 
-    backward(0, True)
-    backward(1, False)
-    take(0)
-    backward(2, False)
-    step(2)
-    take(1)
-    backward(3, False)
-    step(3)
-    take(2)
+    backward(0, True, lambda: None)
+    backward(1, False, lambda: take(0))
+    backward(2, False, lambda: take(1))
+    backward(3, False, lambda: take(2))
 
     dxn = dxn_s[...]
     xhat = xh_s[...]
@@ -434,8 +415,10 @@
     for j, peer in enumerate(talk):
         push(sm_ref.at[2 * peer[2] + peer[3]], sm0.at[j], send_s.at[0], recv_s.at[0], peer)
 
-    step(4)
     take(3)
+    finish(0)
+    first_x = z * (1 - c) + y * c
+    then_x = y * (1 - c) + z * c
     landed(cxf, recv_rx.at[0])
     for b in range(8):
         total = sums[2, 3, b].astype(F32)
@@ -443,13 +426,15 @@
             total = total + cxf[i, b].astype(F32)
         sums[2, 3, b] = total.astype(BF16)
     for d in far_first:
-        push(sums.at[2, 3, shift(z, d, 8)], s2x.at[d - 1], send_2.at[1], recv_2.at[1], line_z[d - 1])
+        to = (lax.rem(z + d * (1 - c), 8), lax.rem(y + d * c, 8), x, c)
+        push(sums.at[2, 3, shift(first_x, d, 8)], s2x.at[d - 1], send_2.at[1], recv_2.at[1], to)
+    finish(1)
     landed(sm0, recv_s.at[0])
     ss1[...] = sm_ref[mp] + sum(sm0[j] for j in range(7))
     for j, to in enumerate(line_y):
         push(ss1, sm1.at[j], send_s.at[1], recv_s.at[1], to)
-    for i in range(4):
-        finish(i)
+    finish(2)
+    finish(3)
     landed(sm1, recv_s.at[1])
     ss2[...] = ss1[...] + sum(sm1[j] for j in range(7))
     for j, to in enumerate(line_z):
@@ -457,6 +442,7 @@
 
     a3[...] = jnp.zeros_like(a3)
     b3[...] = jnp.zeros_like(b3)
+    x3[...] = jnp.zeros_like(x3)
 
     def collect(num, me):
         total = sums[num, 3, me].astype(F32)
@@ -483,15 +469,18 @@
     spread_out(a3, z, r3a, 0, lambda d, core: (shift(z, d, 8), y, x, core))
     collect(1, z)
     for i in range(8):
-        b3[i, 1, 0:12, :] = flat[1, 12 * i : 12 * i + 12, :]
+        b3[i, 0:12, :] = flat[1, 12 * i : 12 * i + 12, :]
+    spread_out(b3, y, r3b, 1, lambda d, core: (z, shift(y, d, 8), x, core))
     landed(s2x, recv_2.at[1])
-    total = sums[2, 3, z].astype(F32)
+    total = sums[2, 3, first_x].astype(F32)
     for j in range(7):
         total = total + s2x[j].astype(F32)
     flat[2] = total
     for i in range(8):
-        b3[i, 0, 0:12, :] = flat[2, 12 * i : 12 * i + 12, :]
-    spread_out(b3, y, r3b, 1, lambda d, core: (z, shift(y, d, 8), x, core))
+        x3[i, 0:12, :] = flat[2, 12 * i : 12 * i + 12, :]
+    spread_out(
+        x3, then_x, r3x, 2, lambda d, core: (lax.rem(z + d * c, 8), lax.rem(y + d * (1 - c), 8), x, core)
+    )
 
     landed(sm2, recv_s.at[2])
     total = ss2[...] + sum(sm2[j] for j in range(7))
@@ -504,9 +493,10 @@
         part_s[core, :, 0:128] = gathered(a3, z, r3a, k)
     landed(r3b, recv_3.at[1])
     for k, core in enumerate((c, 1 - c)):
-        total = gathered(b3, y, r3b, k)
-        part_s[core, :, 128:256] = total[0]
-        part_s[core, :, 256:384] = total[1]
+        part_s[core, :, 256:384] = gathered(b3, y, r3b, k)
+    landed(r3x, recv_3.at[2])
+    for k, core in enumerate((c, 1 - c)):
+        part_s[core, :, 128:256] = gathered(x3, then_x, r3x, k)
     for t in range(4):
         at = 192 * (t % 2)
         both = part_s[t // 2, 0:12, :] * shrink
@@ -525,6 +515,7 @@
     left_here(s2x, send_2.at[1])
     left_here(r3a, send_3.at[0])
     left_here(r3b, send_3.at[1])
+    left_here(r3x, send_3.at[2])
     for k, amount in enumerate((sm0, sm1, sm2)):
         left_here(amount, send_s.at[k])
 
@@ -545,18 +536,19 @@
         out_specs=(VM,) * 6,
         scratch_shapes=[
             b(147, C), b(147, C), pltpu.VMEM((24, 49), jnp.int32), pltpu.VMEM((49, 49), jnp.int32), f(C), f(3, TABLE),
-            f(8, 256), b(4, 4, 2, 96, C), f(8, 8, 256),
+            f(1, C), b(4, 4, 2, 96, C), f(8, 1, C),
             dma((1,)), dma((2,)), dma((2,)), dma((3,)), dma((1,)), dma((4,)), dma((1,)), dma((1,)), dma((10,)),
-            f(152, C), f(192, C), f(192, C), f(192, C), b(192, C), b(C, 384), f(C, 192), b(C, 192),
+            f(152, C), f(192, C), f(192, C), f(192, C), b(192, C), b(C, 384), f(C, 192), b(C, 384),
             f(192, C), f(192, C), b(192, C), f(192, C),
             pltpu.VMEM((64, 128), jnp.int32), f(2, 384, 128), f(4, 64, 384), f(4, 3, 64, 384),
             b(4, 192, 192), b(4, 192, 192), b(4, 192, 192), b(4, 192, 192), f(2, 384, 128), f(8, 8, 384),
-            b(3, 2, 4, 8, 96, 128), b(3, 4, 8, 96, 128), b(2, 2, 4, 96, 128), b(2, 3, 7, 96, 128),
+            b(3, 2, 4, 8, 96, 128), b(3, 4, 8, 96, 128), b(2, 4, 7, 96, 128),
             b(3, 8, 96, 128), b(2, 3, 96, 128), b(7, 96, 128), f(3, 96, 128),
-            f(8, 16, 128), f(8, 2, 16, 128), f(15, 16, 128), f(15, 2, 16, 128), f(2, 16, 384),
+            f(8, 16, 128), f(8, 16, 128), f(8, 16, 128), f(15, 16, 128), f(15, 16, 128), f(15, 16, 128),
+            f(2, 16, 384),
             f(7, 8, 384), f(7, 8, 384), f(7, 8, 384), f(8, 384), f(8, 384),
-            dma((1,)), dma((4,)), dma((1,)), dma((4,)), dma((3,)), dma((1,)), dma((1,)),
-            dma((2,)), dma((2,)), dma((2,)), dma((2,)), dma((3,)), dma((3,)),
+            dma((1,)), dma((4,)), dma((1,)), dma((4,)), dma((1,)), dma((1,)),
+            dma((2,)), dma((2,)), dma((3,)), dma((3,)), dma((3,)), dma((3,)),
         ],
         compiler_params=pltpu.CompilerParams(
             collective_id=0, has_side_effects=True, vmem_limit_bytes=40 * 2**20

time: 73.1 us -> 73.9 us (1.011)
  Pallas kernels: 72.1 us -> 72.9 us
    pallas_call x1, Pallas kernels: 71.3 us -> 72.1 us  [whole(): pl.pallas_call(functools.partial(whole_kernel, count), name='window_layer...]
where the time goes in v5:
time: 73.9 us; the launch traced here: 73.7 us
  Pallas kernels  72.9 us (99%)
  between operations  0.8 us (1%)
    pallas_call x1, Pallas kernels, whole(): pl.pallas_call(functools.partial(whole_kernel, count), name='window_layer...  72.1 us

profile of v5, /device:TPU:1, one launch (start us, length us, event | category | flops | bytes accessed | tf_op | source)
XLA Modules:
  0.0 73.7 jit_solution(10834948633725980506)
XLA Ops:
  0.6 72.1 %window_layer.1 = (f32[147,768]{1,0:T(8,128)S(1)}, f32[3,12,96]{2,1,0:T(8,128)S(1)}, f32[12,96]{1,0:T(8,128)S(1)}, f32[3,169]{1,0:T(4,128)S(1)}, f32[768]{0:T(1024)S(1)}, /*index=5*/f32[1,128]{1,0:T(1,128)S(1)}) custom-call(bf16[147,768]{1,0:T(8,128)(2,1)} %refs_0_.1, bf16[147,768]{1,0:T(8,128)(2,1)} %refs_1_.1, s32[24,49]{1,0:T(8,128)} %refs_2_.1, ...), custom_call_target="tpu_custom_call" | custom-call | tf_op jit(solution)/shard_map/window_layer/pallas_call | solution.py:528
  72.7 0.8 %hand_out.1 = (f32[147,768]{1,0:T(8,128)}, f32[3,12,96]{2,1,0:T(8,128)}, f32[12,96]{1,0:T(8,128)}, f32[3,169]{1,0:T(4,128)}, f32[768]{0:T(1024)}, /*index=5*/f32[1,128]{1,0:T(1,128)}) custom-call(f32[147,768]{1,0:T(8,128)S(1)} %get-tuple-element.18.refs_0_, f32[3,12,96]{2,1,0:T(8,128)S(1)} %get-tuple-element.19.refs_1_, ...), custom_call_target="tpu_custom_call" | custom-call | tf_op jit(solution)/shard_map/hand_out/pallas_call | solution.py:568

commit v6 on v5

--- a/solution.py
+++ b/solution.py
@@ -435,10 +435,6 @@
         push(ss1, sm1.at[j], send_s.at[1], recv_s.at[1], to)
     finish(2)
     finish(3)
-    landed(sm1, recv_s.at[1])
-    ss2[...] = ss1[...] + sum(sm1[j] for j in range(7))
-    for j, to in enumerate(line_z):
-        push(ss2, sm2.at[j], send_s.at[2], recv_s.at[2], to)
 
     a3[...] = jnp.zeros_like(a3)
     b3[...] = jnp.zeros_like(b3)
@@ -482,12 +478,10 @@
         x3, then_x, r3x, 2, lambda d, core: (lax.rem(z + d * c, 8), lax.rem(y + d * (1 - c), 8), x, core)
     )
 
-    landed(sm2, recv_s.at[2])
-    total = ss2[...] + sum(sm2[j] for j in range(7))
-    gtab_ref[...] = total[0:3, 0:TABLE] * shrink
-    for j in range(6):
-        ggain_ref[pl.ds(128 * j, 128)] = total[j : j + 1, 256:384].reshape(128) * shrink
-    loss_ref[...] = total[6:7, 256:384] * (0.5 / count)
+    landed(sm1, recv_s.at[1])
+    ss2[...] = ss1[...] + sum(sm1[j] for j in range(7))
+    for j, to in enumerate(line_z):
+        push(ss2, sm2.at[j], send_s.at[2], recv_s.at[2], to)
     landed(r3a, recv_3.at[0])
     for k, core in enumerate((c, 1 - c)):
         part_s[core, :, 0:128] = gathered(a3, z, r3a, k)
@@ -505,6 +499,12 @@
             gq_ref[t] = mine
         else:
             gp_ref[...] = mine
+    landed(sm2, recv_s.at[2])
+    total = ss2[...] + sum(sm2[j] for j in range(7))
+    gtab_ref[...] = total[0:3, 0:TABLE] * shrink
+    for j in range(6):
+        ggain_ref[pl.ds(128 * j, 128)] = total[j : j + 1, 256:384].reshape(128) * shrink
+    loss_ref[...] = total[6:7, 256:384] * (0.5 / count)
     left_here(w_ref.at[:, pl.ds(0, 3), 0], send_w.at[0])
     left_here(w_ref.at[:, :, 0], send_c.at[0])
     left_here(t_ref.at[pl.ds(0, 7)], send_t.at[0])

time: 73.9 us -> 70.1 us (0.949)
  Pallas kernels: 72.9 us -> 69.1 us
    pallas_call x1, Pallas kernels: 72.1 us -> 68.3 us  [whole(): pl.pallas_call(functools.partial(whole_kernel, count), name='window_layer...]
where the time goes in v6:
time: 70.1 us; the launch traced here: 69.9 us
  Pallas kernels  69.1 us (99%)
  between operations  0.8 us (1%)
    pallas_call x1, Pallas kernels, whole(): pl.pallas_call(functools.partial(whole_kernel, count), name='window_layer...  68.3 us

profile of v6, /device:TPU:1, one launch (start us, length us, event | category | flops | bytes accessed | tf_op | source)
XLA Modules:
  0.0 69.9 jit_solution(14078323786768026753)
XLA Ops:
  0.6 68.3 %window_layer.1 = (f32[147,768]{1,0:T(8,128)S(1)}, f32[3,12,96]{2,1,0:T(8,128)S(1)}, f32[12,96]{1,0:T(8,128)S(1)}, f32[3,169]{1,0:T(4,128)S(1)}, f32[768]{0:T(1024)S(1)}, /*index=5*/f32[1,128]{1,0:T(1,128)S(1)}) custom-call(bf16[147,768]{1,0:T(8,128)(2,1)} %refs_0_.1, bf16[147,768]{1,0:T(8,128)(2,1)} %refs_1_.1, s32[24,49]{1,0:T(8,128)} %refs_2_.1, ...), custom_call_target="tpu_custom_call" | custom-call | tf_op jit(solution)/shard_map/window_layer/pallas_call | solution.py:528
  68.9 0.8 %hand_out.1 = (f32[147,768]{1,0:T(8,128)}, f32[3,12,96]{2,1,0:T(8,128)}, f32[12,96]{1,0:T(8,128)}, f32[3,169]{1,0:T(4,128)}, f32[768]{0:T(1024)}, /*index=5*/f32[1,128]{1,0:T(1,128)}) custom-call(f32[147,768]{1,0:T(8,128)S(1)} %get-tuple-element.18.refs_0_, f32[3,12,96]{2,1,0:T(8,128)S(1)} %get-tuple-element.19.refs_1_, ...), custom_call_target="tpu_custom_call" | custom-call | tf_op jit(solution)/shard_map/hand_out/pallas_call | solution.py:568

commit v7 on v6

--- a/solution.py
+++ b/solution.py
@@ -147,7 +147,7 @@
 
     xt = jnp.transpose(xn_s[...].astype(F32))
     xt_s[:, 0:192] = xt.astype(BF16)
-    xtf_s[...] = xt
+    xtf_s[0:C, :] = xt
     for b in range(8):
         block = jnp.concatenate([xtf_s[96 * k + 12 * b : 96 * k + 12 * b + 12, :] for k in range(8)], axis=0)
         xtp_s[96 * b : 96 * b + 96, 0:192] = block.astype(BF16)
@@ -291,7 +291,7 @@
     gb_s[...] = err.astype(BF16)
     turned = jnp.transpose(err)
     xt_s[:, 192:384] = turned.astype(BF16)
-    xtf_s[...] = turned
+    xtf_s[0:C, :] = turned
     for b in range(8):
         block = jnp.concatenate([xtf_s[96 * k + 12 * b : 96 * k + 12 * b + 12, :] for k in range(8)], axis=0)
         xtp_s[96 * b : 96 * b + 96, 192:384] = block.astype(BF16)
@@ -389,7 +389,8 @@
     m2 = jnp.sum(dxh * xhat, axis=1, keepdims=True) * (1.0 / C)
     out = err_s[...] + inv * (dxh - m1 - xhat * m2)
     for w in range(3):
-        gi_ref[49 * w : 49 * w + 49, :] = out[64 * w : 64 * w + 49, :]
+        pad_s[49 * w : 49 * w + 49, :] = out[64 * w : 64 * w + 49, :]
+    gi_ref[...] = pad_s[0:147, :]
     gain = jnp.sum(dxn * xhat, axis=0, keepdims=True)
     sq = err_s[...]
     loss = jnp.sum(sq * sq, axis=0, keepdims=True)
@@ -444,7 +445,7 @@
         total = sums[num, 3, me].astype(F32)
         for i in range(3):
             total = total + s2[num, i].astype(F32)
-        flat[num] = total
+        flat[num, 0:96, :] = total
 
     def spread_out(src, me, dst, num, reach):
         for d in (4, 3, 5, 2, 6, 1, 7, 0):
@@ -471,7 +472,7 @@
     total = sums[2, 3, first_x].astype(F32)
     for j in range(7):
         total = total + s2x[j].astype(F32)
-    flat[2] = total
+    flat[2, 0:96, :] = total
     for i in range(8):
         x3[i, 0:12, :] = flat[2, 12 * i : 12 * i + 12, :]
     spread_out(
@@ -538,12 +539,12 @@
             b(147, C), b(147, C), pltpu.VMEM((24, 49), jnp.int32), pltpu.VMEM((49, 49), jnp.int32), f(C), f(3, TABLE),
             f(1, C), b(4, 4, 2, 96, C), f(8, 1, C),
             dma((1,)), dma((2,)), dma((2,)), dma((3,)), dma((1,)), dma((4,)), dma((1,)), dma((1,)), dma((10,)),
-            f(152, C), f(192, C), f(192, C), f(192, C), b(192, C), b(C, 384), f(C, 192), b(C, 384),
+            f(160, C), f(192, C), f(192, C), f(192, C), b(192, C), b(C, 384), f(C + 8, 192), b(C, 384),
             f(192, C), f(192, C), b(192, C), f(192, C),
             pltpu.VMEM((64, 128), jnp.int32), f(2, 384, 128), f(4, 64, 384), f(4, 3, 64, 384),
             b(4, 192, 192), b(4, 192, 192), b(4, 192, 192), b(4, 192, 192), f(2, 384, 128), f(8, 8, 384),
             b(3, 2, 4, 8, 96, 128), b(3, 4, 8, 96, 128), b(2, 4, 7, 96, 128),
-            b(3, 8, 96, 128), b(2, 3, 96, 128), b(7, 96, 128), f(3, 96, 128),
+            b(3, 8, 96, 128), b(2, 3, 96, 128), b(7, 96, 128), f(3, 104, 128),
             f(8, 16, 128), f(8, 16, 128), f(8, 16, 128), f(15, 16, 128), f(15, 16, 128), f(15, 16, 128),
             f(2, 16, 384),
             f(7, 8, 384), f(7, 8, 384), f(7, 8, 384), f(8, 384), f(8, 384),

time: 70.1 us -> 70 us (level)
  no operation moved by 1% of the time
where the time goes in v7:
time: 70 us; the launch traced here: 69.9 us
  Pallas kernels  69.1 us (99%)
  between operations  0.8 us (1%)
    pallas_call x1, Pallas kernels, whole(): pl.pallas_call(functools.partial(whole_kernel, count), name='window_layer...  68.3 us

profile of v7, /device:TPU:1, one launch (start us, length us, event | category | flops | bytes accessed | tf_op | source)
XLA Modules:
  0.0 69.9 jit_solution(7250325471255440306)
XLA Ops:
  0.6 68.3 %window_layer.1 = (f32[147,768]{1,0:T(8,128)S(1)}, f32[3,12,96]{2,1,0:T(8,128)S(1)}, f32[12,96]{1,0:T(8,128)S(1)}, f32[3,169]{1,0:T(4,128)S(1)}, f32[768]{0:T(1024)S(1)}, /*index=5*/f32[1,128]{1,0:T(1,128)S(1)}) custom-call(bf16[147,768]{1,0:T(8,128)(2,1)} %refs_0_.1, bf16[147,768]{1,0:T(8,128)(2,1)} %refs_1_.1, s32[24,49]{1,0:T(8,128)} %refs_2_.1, ...), custom_call_target="tpu_custom_call" | custom-call | tf_op jit(solution)/shard_map/window_layer/pallas_call | solution.py:529
  68.9 0.8 %hand_out.1 = (f32[147,768]{1,0:T(8,128)}, f32[3,12,96]{2,1,0:T(8,128)}, f32[12,96]{1,0:T(8,128)}, f32[3,169]{1,0:T(4,128)}, f32[768]{0:T(1024)}, /*index=5*/f32[1,128]{1,0:T(1,128)}) custom-call(f32[147,768]{1,0:T(8,128)S(1)} %get-tuple-element.18.refs_0_, f32[3,12,96]{2,1,0:T(8,128)S(1)} %get-tuple-element.19.refs_1_, ...), custom_call_target="tpu_custom_call" | custom-call | tf_op jit(solution)/shard_map/hand_out/pallas_call | solution.py:569
